TPU v7x, 256 devices: a whole 4x4x8 slice. The times are simulated.
256 devices in a mesh: rep: 1, r: 32 (over y, z), s: 8 (over x, core).
Axes of the slice: x: 4, y: 4, z: 8, core: 2. Of those that a mesh axis runs over, the one named last changes fastest.
Arguments:
- x: bfloat16 [256, 2048, 896], P(('rep', 'r', 's'))
- dy: bfloat16 [256, 2048, 896], P(('rep', 'r', 's'))
- w_gate: bfloat16 [2, 896, 3584], P(None, 's')
- w_up: bfloat16 [2, 896, 3584], P(None, 's')
- w_down: bfloat16 [2, 3584, 896], P(None, 's')
- m_w_gate: float32 [2, 896, 3584], P(None, 's')
- m_w_up: float32 [2, 896, 3584], P(None, 's')
- m_w_down: float32 [2, 3584, 896], P(None, 's')
- v_w_gate: float32 [2, 896, 3584], P(None, 's')
- v_w_up: float32 [2, 896, 3584], P(None, 's')
- v_w_down: float32 [2, 3584, 896], P(None, 's')
Outputs:
- output 1: bfloat16 [2, 896, 3584], P('rep', 's')
- output 2: bfloat16 [2, 896, 3584], P('rep', 's')
- output 3: bfloat16 [2, 3584, 896], P('rep', 's')
- output 4: float32 [2, 896, 3584], P('rep', 's')
- output 5: float32 [2, 896, 3584], P('rep', 's')
- output 6: float32 [2, 3584, 896], P('rep', 's')
- output 7: float32 [2, 896, 3584], P('rep', 's')
- output 8: float32 [2, 896, 3584], P('rep', 's')
- output 9: float32 [2, 3584, 896], P('rep', 's')
All inputs are finite; a program needn't handle non-finite values.
Results may differ from a plain program's by a relative error of at most 0.022.
Values are sent between devices in bfloat16 or wider.
A program may use at most 768 MiB of HBM per device.

v0:
```python
import jax
import jax.numpy as jnp
from jax import lax
from jax.sharding import PartitionSpec as P

NAMES = ("w_gate", "w_up", "w_down")


def matmul(a, w):
    return jnp.dot(a, w, preferred_element_type=jnp.float32).astype(jnp.bfloat16)


def normed(h):
    wide = h.astype(jnp.float32)
    scale = lax.rsqrt(jnp.mean(wide**2, -1, keepdims=True) + 1e-6)
    return (wide * scale).astype(jnp.bfloat16)


def layer(h, w):
    a = normed(h)
    gate = jnp.dot(a, w["w_gate"], preferred_element_type=jnp.float32)
    up = jnp.dot(a, w["w_up"], preferred_element_type=jnp.float32)
    return h + matmul((jax.nn.silu(gate) * up).astype(jnp.bfloat16), w["w_down"])


def adamw(w, m, v, g):
    m = 0.9 * m + 0.1 * g
    v = 0.95 * v + 0.05 * g * g
    step = m * lax.rsqrt(v + 1e-8) + 0.1 * w
    return (w - 0.02 * step).astype(jnp.bfloat16), m, v


def clipped(gradients, sum_of_squares, count):
    factor = jnp.minimum(1.0, 0.5 * lax.rsqrt(sum_of_squares / count + 1e-30))
    return [g * factor for g in gradients]


def solution(mesh):
    def fetched(weights, number):
        return {name: lax.all_gather(w[number], "s", axis=0, tiled=True) for name, w in zip(NAMES, weights, strict=True)}

    def summed(term):
        return lax.psum(lax.psum_scatter(term, "s", scatter_dimension=0, tiled=True), "r")

    def step(x, dy, *arrays):
        weights, m, v = (arrays[i : i + 3] for i in (0, 3, 6))
        layers = weights[0].shape[0]
        h, kept = x[0], []
        for number in range(layers):
            kept.append(h)
            h = layer(h, fetched(weights, number))
        by_h, mine = dy[0], [None] * layers
        for number in reversed(range(layers)):
            _, back = jax.vjp(lambda w, h: layer(h, w), fetched(weights, number), kept[number])
            by_w, by_h = back(by_h)
            mine[number] = [summed(by_w[name]) for name in NAMES]
        gradients = [jnp.stack([mine[number][i] for number in range(layers)]).astype(jnp.float32) for i in range(3)]
        squares = lax.psum(sum(jnp.sum(g * g) for g in gradients), "s")
        gradients = clipped(gradients, squares, lax.psum(1, "s") * sum(g.size for g in gradients))
        new = [adamw(w.astype(jnp.float32), m, v, g) for w, m, v, g in zip(weights, m, v, gradients, strict=True)]
        return tuple(one[which] for which in range(3) for one in new)

    states, cut = P(("rep", "r", "s"), None, None), P(None, "s", None)
    return jax.shard_map(
        step,
        mesh=mesh,
        in_specs=(states, states) + (cut,) * 9,
        out_specs=(P("rep", "s", None),) * 9,
        check_vma=False,
    )
```

profile of v0, /device:TPU:1, one launch (start us, length us, event | category | flops | bytes accessed | tf_op | source)
XLA Modules:
  0.0 908.1 jit_solution(13382825735924067419)
XLA Ops:
  7.2 2.7 fusion.94
  10.1 2.6 fusion.93
  12.8 1.3 fusion.92
  14.1 0.5 all-gather.21.cloned.1.call-update
  14.7 0.5 all-gather.23.cloned.1.call-update
  15.3 0.5 all-gather.19.cloned.1.call-update
  15.9 6.2 copy.20
  22.1 2.8 fusion.15
  24.9 6.1 copy.21
  31.0 27.3 %all-gather.13.cloned.1.call-done = bf16[1,896,3584]{2,1,0:T(8,128)(2,1)} async-done(((bf16[1,112,3584]{2,1,0:T(8,128)(2,1)}), bf16[1,896,3584]{2,1,0:T(8,128)(2,1)}) %all-gather.13.cloned.1.call-update) | async-done | bytes 6422544 | tf_op jit(solution)/shard_map/all_gather | solution.py:40
  58.3 24.1 %fusion.41 = f32[2048,3584]{1,0:T(8,128)} fusion(bf16[1,896,3584]{2,1,0:T(8,128)(2,1)} %all-gather.13.cloned.1.call-done, bf16[1,2048,896]{1,2,0:T(8,128)(2,1)} %copy.20, f32[2048]{0:T(1024)S(1)} %add_rsqrt_fusion), kind=kOutput, calls=%fused_computation.59 | convolution fusion | flops 13158842368 | bytes 39460864 | tf_op jit(solution)/shard_map/dot_general | solution.py:21
  82.4 22.2 %all-gather.15.cloned.1.call-done = bf16[1,896,3584]{2,1,0:T(8,128)(2,1)} async-done(((bf16[1,112,3584]{2,1,0:T(8,128)(2,1)}), bf16[1,896,3584]{2,1,0:T(8,128)(2,1)}) %all-gather.15.cloned.1.call-update) | async-done | bytes 6422544 | tf_op jit(solution)/shard_map/all_gather | solution.py:40
  104.6 33.8 %multiply_convert_fusion.1 = (bf16[2048,3584]{1,0:T(8,128)(2,1)}, f32[2048,3584]{1,0:T(8,128)}) fusion(f32[2048,3584]{1,0:T(8,128)} %fusion.41, bf16[1,896,3584]{2,1,0:T(8,128)(2,1)} %all-gather.15.cloned.1.call-done, bf16[1,2048,896]{1,2,0:T(8,128)(2,1)} %copy.20, f32[2048]{0:T(1024)S(1)} %add_rsqrt_fusion), kind=kOutput, calls=%fused_computation.17 | convolution fusion | flops 13202882560 | bytes 83501056 | tf_op jit(solution)/shard_map/dot_general | solution.py:22
  138.4 12.5 %all-gather.17.cloned.1.call-done = bf16[1,3584,896]{2,1,0:T(8,128)(2,1)} async-done(((bf16[1,448,896]{2,1,0:T(8,128)(2,1)}), bf16[1,3584,896]{2,1,0:T(8,128)(2,1)}) %all-gather.17.cloned.1.call-update) | async-done | bytes 6422544 | tf_op jit(solution)/shard_map/all_gather | solution.py:40
  150.9 21.1 %fusion.19 = (f32[2048]{0:T(1024)S(1)}, bf16[2048,896]{0,1:T(8,128)(2,1)}) fusion(bf16[2048,3584]{1,0:T(8,128)(2,1)} %get-tuple-element.30, bf16[1,3584,896]{2,1,0:T(8,128)(2,1)} %all-gather.17.cloned.1.call-done, bf16[1,2048,896]{1,2,0:T(8,128)(2,1)} %copy.20), kind=kOutput, calls=%fused_computation.37 | convolution fusion | flops 13162510336 | bytes 28450816 | tf_op jit(solution)/shard_map/dot_general | solution.py:10
  172.1 25.0 %all-gather.21.cloned.1.call-done = bf16[1,3584,896]{2,1,0:T(8,128)(2,1)} async-done(((bf16[1,448,896]{2,1,0:T(8,128)(2,1)}), bf16[1,3584,896]{2,1,0:T(8,128)(2,1)}) %all-gather.21.cloned.1.call-update) | async-done | bytes 6422544 | tf_op jit(solution)/shard_map/all_gather | solution.py:40
  197.1 22.1 %convolution_convert_fusion.1 = bf16[2048,3584]{1,0:T(8,128)(2,1)} fusion(bf16[1,3584,896]{2,1,0:T(8,128)(2,1)} %all-gather.21.cloned.1.call-done, bf16[1,2048,896]{2,1,0:T(8,128)(2,1)} %param.12), kind=kOutput, calls=%fused_computation.23 | convolution fusion | flops 13160677376 | bytes 24772608 | tf_op jit(solution)/shard_map/transpose(jvp())/dot_general | solution.py:10
  219.2 24.1 %all-gather.23.cloned.1.call-done = bf16[1,896,3584]{2,1,0:T(8,128)(2,1)} async-done(((bf16[1,112,3584]{2,1,0:T(8,128)(2,1)}), bf16[1,896,3584]{2,1,0:T(8,128)(2,1)}) %all-gather.23.cloned.1.call-update) | async-done | bytes 6422544 | tf_op jit(solution)/shard_map/all_gather | solution.py:40
  243.3 24.1 %fusion.28 = f32[2048,3584]{1,0:T(8,128)} fusion(bf16[1,896,3584]{2,1,0:T(8,128)(2,1)} %all-gather.23.cloned.1.call-done, bf16[2048,896]{0,1:T(8,128)(2,1)} %get-tuple-element.33, f32[2048]{0:T(1024)S(1)} %fusion.80), kind=kOutput, calls=%fused_computation.46 | convolution fusion | flops 13158842368 | bytes 39460864 | tf_op jit(solution)/shard_map/jvp()/dot_general | solution.py:22
  267.4 22.1 %all-gather.19.cloned.1.call-done = bf16[1,896,3584]{2,1,0:T(8,128)(2,1)} async-done(((bf16[1,112,3584]{2,1,0:T(8,128)(2,1)}), bf16[1,896,3584]{2,1,0:T(8,128)(2,1)}) %all-gather.19.cloned.1.call-update) | async-done | bytes 6422544 | tf_op jit(solution)/shard_map/all_gather | solution.py:40
  289.5 42.9 %fusion.2 = (bf16[2048,3584]{1,0:T(8,128)(2,1)}, f32[2048,3584]{1,0:T(8,128)}) fusion(f32[2048,3584]{1,0:T(8,128)} %fusion.28, bf16[2048,3584]{1,0:T(8,128)(2,1)} %convolution_convert_fusion.1, bf16[1,896,3584]{2,1,0:T(8,128)(2,1)} %all-gather.19.cloned.1.call-done, bf16[2048,896]{0,1:T(8,128)(2,1)} %get-tuple-element.33, f32[2048]{0:T(1024)S(1)} %fusion.80), kind=kOutput, calls=%fused_computation.8 | convolution fusion | flops 13246922752 | bytes 98181120 | tf_op jit(solution)/shard_map/jvp()/dot_general | solution.py:21
  332.3 22.7 %fusion.12 = bf16[2048,896]{0,1:T(8,128)(2,1)} fusion(bf16[2048,3584]{1,0:T(8,128)(2,1)} %convolution_convert_fusion.1, bf16[1,896,3584]{2,1,0:T(8,128)(2,1)} %all-gather.23.cloned.1.call-done, f32[2048,3584]{1,0:T(8,128)} %get-tuple-element.35), kind=kOutput, calls=%fused_computation.21 | convolution fusion | flops 13197377536 | bytes 54132736 | tf_op jit(solution)/shard_map/transpose(jvp())/dot_general | solution.py:22
  355.0 19.9 %fusion.21 = (f32[2048]{0:T(1024)S(1)}, bf16[2048,896]{0,1:T(8,128)(2,1)S(1)}) fusion(bf16[2048,896]{0,1:T(8,128)(2,1)S(1)} %copy-done.5, bf16[2048,896]{0,1:T(8,128)(2,1)} %fusion.12, bf16[2048,3584]{1,0:T(8,128)(2,1)} %get-tuple-element.34, bf16[1,896,3584]{2,1,0:T(8,128)(2,1)} %all-gather.19.cloned.1.call-done), kind=kOutput, calls=%fused_computation.39 | convolution fusion | flops 13162510336 | bytes 32120832 | tf_op jit(solution)/shard_map/transpose(jvp())/dot_general | solution.py:21
  375.0 3.0 fusion.47
  378.0 1.8 copy-done.6
  379.8 19.4 %convolution_convert_fusion.2 = bf16[3584,896]{1,0:T(8,128)(2,1)} fusion(bf16[2048,3584]{1,0:T(8,128)(2,1)} %get-tuple-element.30, bf16[2048,896]{0,1:T(8,128)(2,1)S(1)} %fusion.47), kind=kOutput, calls=%fused_computation.43 | convolution fusion | flops 13156548608 | bytes 24772608 | tf_op jit(solution)/shard_map/transpose(jvp())/dot_general | solution.py:10
  399.3 26.8 %fusion.22 = bf16[3584,896]{1,0:T(8,128)(2,1)} fusion(f32[2048,3584]{1,0:T(8,128)} %fusion.28, bf16[1,2048,896]{2,1,0:T(8,128)(2,1)} %param.12, f32[2048,3584]{1,0:T(8,128)} %get-tuple-element.35), kind=kOutput, calls=%fused_computation.40 | convolution fusion | flops 13200588800 | bytes 68812800 | tf_op jit(solution)/shard_map/transpose(jvp())/dot_general | solution.py:10
  426.2 22.0 %convolution_convert_fusion = bf16[2048,3584]{1,0:T(8,128)(2,1)} fusion(bf16[2048,896]{0,1:T(8,128)(2,1)} %copy-done.6, bf16[1,3584,896]{2,1,0:T(8,128)(2,1)} %all-gather.17.cloned.1.call-done), kind=kOutput, calls=%fused_computation.22 | convolution fusion | flops 13160677376 | bytes 24772608 | tf_op jit(solution)/shard_map/transpose(jvp())/dot_general | solution.py:10
  448.2 24.3 %fusion.24 = bf16[896,3584]{1,0:T(8,128)(2,1)} fusion(bf16[2048,3584]{1,0:T(8,128)(2,1)} %convolution_convert_fusion, f32[2048,3584]{1,0:T(8,128)} %fusion.41, bf16[1,2048,896]{1,2,0:T(8,128)(2,1)} %copy.20, f32[2048]{0:T(1024)S(1)} %copy-done.19), kind=kOutput, calls=%fused_computation.42 | convolution fusion | flops 13206093824 | bytes 54140928 | tf_op jit(solution)/shard_map/transpose(jvp())/dot_general | solution.py:22
  472.6 0.6 copy-done.15
  473.2 24.0 %fusion.23 = bf16[896,3584]{1,0:T(8,128)(2,1)} fusion(bf16[2048,3584]{1,0:T(8,128)(2,1)} %convolution_convert_fusion.1, bf16[2048,896]{0,1:T(8,128)(2,1)} %get-tuple-element.33, f32[2048]{0:T(1024)S(1)} %copy-done.15, f32[2048,3584]{1,0:T(8,128)} %get-tuple-element.35), kind=kOutput, calls=%fused_computation.41 | convolution fusion | flops 13206093824 | bytes 54140928 | tf_op jit(solution)/shard_map/transpose(jvp())/dot_general | solution.py:22
  497.2 33.4 %fusion.25 = bf16[896,3584]{1,0:T(8,128)(2,1)} fusion(f32[2048,3584]{1,0:T(8,128)} %fusion.41, f32[2048,3584]{1,0:T(8,128)} %get-tuple-element.31, bf16[2048,3584]{1,0:T(8,128)(2,1)} %convolution_convert_fusion, bf16[1,2048,896]{1,2,0:T(8,128)(2,1)} %copy.20, f32[2048]{0:T(1024)S(1)} %copy-done.19), kind=kOutput, calls=%fused_computation.45 | convolution fusion | flops 13242793984 | bytes 83501056 | tf_op jit(solution)/shard_map/transpose(jvp())/dot_general | solution.py:21
  530.7 19.4 %convolution_convert_fusion.3 = bf16[896,3584]{1,0:T(8,128)(2,1)} fusion(bf16[2048,3584]{1,0:T(8,128)(2,1)} %get-tuple-element.34, bf16[2048,896]{0,1:T(8,128)(2,1)} %get-tuple-element.33, f32[2048]{0:T(1024)S(1)} %copy-done.15), kind=kOutput, calls=%fused_computation.44 | convolution fusion | flops 13158842368 | bytes 24780800 | tf_op jit(solution)/shard_map/transpose(jvp())/dot_general | solution.py:21
  550.3 38.0 %reduce-scatter.13.cloned.1.call-done = bf16[112,3584]{1,0:T(8,128)(2,1)} async-done(((bf16[896,3584]{1,0:T(8,128)(2,1)}), bf16[112,3584]{1,0:T(8,128)(2,1)}) %reduce-scatter.13.cloned.1.call-update) | async-done | bytes 802832 | tf_op jit(solution)/shard_map/reduce_scatter | solution.py:43
  588.4 48.0 %reduce-scatter.7.cloned.1.call-done = bf16[112,3584]{1,0:T(8,128)(2,1)} async-done(((bf16[896,3584]{1,0:T(8,128)(2,1)}), bf16[112,3584]{1,0:T(8,128)(2,1)}) %reduce-scatter.7.cloned.1.call-update) | async-done | bytes 802832 | tf_op jit(solution)/shard_map/reduce_scatter | solution.py:43
  636.4 47.9 %reduce-scatter.9.cloned.1.call-done = bf16[112,3584]{1,0:T(8,128)(2,1)} async-done(((bf16[896,3584]{1,0:T(8,128)(2,1)}), bf16[112,3584]{1,0:T(8,128)(2,1)}) %reduce-scatter.9.cloned.1.call-update) | async-done | bytes 802832 | tf_op jit(solution)/shard_map/reduce_scatter | solution.py:43
  684.3 171.6 %all-reduce.3.cloned.1.call-done = (bf16[1,112,3584]{2,1,0:T(8,128)(2,1)}, bf16[1,112,3584]{2,1,0:T(8,128)(2,1)}, bf16[1,112,3584]{2,1,0:T(8,128)(2,1)}, bf16[1,...) async-done(((bf16[1,112,3584]{2,1,0:T(8,128)(2,1)}, bf16[1,112,3584]{2,1,0:T(8,128)(2,1)}, bf16[1,112,3584]{2,1,0:T(8,128)(2,1)}, ...) | async-done | bytes 4816912 | tf_op jit(solution)/shard_map/psum | solution.py:43
  855.9 2.8 fusion.62
  858.7 2.8 fusion.61
  861.5 2.9 fusion.60
  866.4 14.6 %psum.55 = f32[]{:T(128)} all-reduce(f32[]{:T(128)S(6)} %add.111), channel_id=1, replica_groups=mesh['rep'=1,'r'=32,'s'=8] {'s'}, use_global_device_ids=true, to_apply=%region_18.19 | all-reduce | flops 1 | bytes 8 | tf_op jit(solution)/shard_map/psum | solution.py:58
  881.8 7.2 fusion.68
  889.1 0.2 copy-done.7
  889.2 1.5 copy-done.8
  890.7 0.9 copy-done.9
  891.6 0.9 copy-done.10
  892.7 0.2 copy-done.12
  892.9 8.5 fusion.59
  (62 shorter events, 1.0 us)
Async XLA Ops:
  7.2 5.6 copy-start.3
  7.2 51.1 %all-gather.13.cloned.1.call-start = ((), (), s32[]{:S(2)}) async-start(), calls=%async_computation.12 | async-start | bytes 7225344 | tf_op jit(solution)/shard_map/all_gather | solution.py:40
  10.0 94.6 %all-gather.15.cloned.1.call-start = ((), (), s32[]{:S(2)}) async-start(), calls=%async_computation.13 | async-start | bytes 7225344 | tf_op jit(solution)/shard_map/all_gather | solution.py:40
  12.7 138.2 %all-gather.17.cloned.1.call-start = ((), (), s32[]{:S(2)}) async-start(), calls=%async_computation.14 | async-start | bytes 7225344 | tf_op jit(solution)/shard_map/all_gather | solution.py:40
  14.1 183.0 %all-gather.21.cloned.1.call-start = ((), (), s32[]{:S(2)}) async-start(), calls=%async_computation.16 | async-start | bytes 7225344 | tf_op jit(solution)/shard_map/all_gather | solution.py:40
  14.7 228.7 %all-gather.23.cloned.1.call-start = ((), (), s32[]{:S(2)}) async-start(), calls=%async_computation.17 | async-start | bytes 7225344 | tf_op jit(solution)/shard_map/all_gather | solution.py:40
  15.2 274.2 %all-gather.19.cloned.1.call-start = ((), (), s32[]{:S(2)}) async-start(), calls=%async_computation.15 | async-start | bytes 7225344 | tf_op jit(solution)/shard_map/all_gather | solution.py:40
  15.8 534.4 %reduce-scatter.15.cloned.1.call-start = ((), (), s32[]{:S(2)}) async-start(), calls=%async_computation.10 | async-start | bytes 7225344 | tf_op jit(solution)/shard_map/reduce_scatter | solution.py:43
  24.9 79.7 %copy-start.18 = (f32[2048]{0:T(1024)}, f32[2048]{0:T(1024)S(1)}, u32[]{:S(2)}) copy-start(f32[2048]{0:T(1024)S(1)} %add_rsqrt_fusion) | copy-start | bytes 24580
  172.1 47.1 %copy-start.16 = (f32[2048]{0:T(1024)}, f32[2048]{0:T(1024)S(1)}, u32[]{:S(2)}) copy-start(f32[2048]{0:T(1024)S(1)} %get-tuple-element.32) | copy-start | bytes 24580
  172.1 202.9 %copy-start.14 = (f32[2048]{0:T(1024)}, f32[2048]{0:T(1024)S(1)}, u32[]{:S(2)}) copy-start(f32[2048]{0:T(1024)S(1)} %fusion.80) | copy-start | bytes 24580
  332.3 22.7 %copy-start.5 = (bf16[2048,896]{0,1:T(8,128)(2,1)S(1)}, bf16[2048,896]{0,1:T(8,128)(2,1)}, u32[]{:S(2)}) copy-start(bf16[2048,896]{0,1:T(8,128)(2,1)} %get-tuple-element.33) | copy-start | bytes 11010052
  355.0 19.9 %copy-start.17 = (f32[2048]{0:T(1024)S(1)}, f32[2048]{0:T(1024)}, u32[]{:S(2)}) copy-start(f32[2048]{0:T(1024)} %copy-done.16) | copy-start | bytes 24580
  355.0 20.0 %copy-start = (bf16[1,2048,896]{1,2,0:T(8,128)(2,1)S(1)}, bf16[1,2048,896]{1,2,0:T(8,128)(2,1)}, u32[]{:S(2)}) copy-start(bf16[1,2048,896]{1,2,0:T(8,128)(2,1)} %copy.21) | copy-start | bytes 11010052
  378.0 1.8 copy-start.6
  399.3 151.0 %reduce-scatter.17.cloned.1.call-start = ((), (), s32[]{:S(2)}) async-start(), calls=%async_computation.11 | async-start | bytes 7225344 | tf_op jit(solution)/shard_map/reduce_scatter | solution.py:43
  426.1 22.1 %copy-start.19 = (f32[2048]{0:T(1024)S(1)}, f32[2048]{0:T(1024)}, u32[]{:S(2)}) copy-start(f32[2048]{0:T(1024)} %copy-done.18) | copy-start | bytes 24580
  426.1 124.2 %reduce-scatter.11.cloned.1.call-start = ((), (), s32[]{:S(2)}) async-start(), calls=%async_computation.8 | async-start | bytes 7225344 | tf_op jit(solution)/shard_map/reduce_scatter | solution.py:43
  472.5 0.7 copy-start.15
  472.5 115.8 %reduce-scatter.13.cloned.1.call-start = ((), (), s32[]{:S(2)}) async-start(), calls=%async_computation.9 | async-start | bytes 7225344 | tf_op jit(solution)/shard_map/reduce_scatter | solution.py:43
  497.2 139.2 %reduce-scatter.7.cloned.1.call-start = ((), (), s32[]{:S(2)}) async-start(), calls=%async_computation.6 | async-start | bytes 7225344 | tf_op jit(solution)/shard_map/reduce_scatter | solution.py:43
  530.7 153.6 %reduce-scatter.9.cloned.1.call-start = ((), (), s32[]{:S(2)}) async-start(), calls=%async_computation.7 | async-start | bytes 7225344 | tf_op jit(solution)/shard_map/reduce_scatter | solution.py:43
  550.2 331.5 %copy-start.4 = (bf16[2,448,896]{2,1,0:T(8,128)(2,1)S(1)}, bf16[2,448,896]{2,1,0:T(8,128)(2,1)}, u32[]{:S(2)}) copy-start(bf16[2,448,896]{2,1,0:T(8,128)(2,1)} %param.15) | copy-start | bytes 4816900
  550.2 305.7 %all-reduce.3.cloned.1.call-start = ((), (), s32[]{:S(2)}) async-start(), calls=%async_computation.18 | async-start | bytes 9633792 | tf_op jit(solution)/shard_map/psum | solution.py:43
  861.5 27.5 %copy-start.13 = (bf16[1,112,3584]{2,1,0:T(8,128)(2,1)S(1)}, bf16[1,112,3584]{2,1,0:T(8,128)(2,1)}, u32[]{:S(2)}) copy-start(bf16[1,112,3584]{2,1,0:T(8,128)(2,1)} %get-tuple-element.11) | copy-start | bytes 2408452
  881.7 7.3 copy-start.1
  881.7 7.3 copy-start.2
  881.7 7.5 copy-start.7
  881.7 9.0 copy-start.8
  881.7 9.9 %copy-start.9 = (f32[2,112,3584]{2,1,0:T(8,128)S(1)}, f32[2,112,3584]{2,1,0:T(8,128)}, u32[]{:S(2)}) copy-start(f32[2,112,3584]{2,1,0:T(8,128)} %param.20) | copy-start | bytes 9633796
  881.8 10.8 %copy-start.10 = (f32[2,112,3584]{2,1,0:T(8,128)S(1)}, f32[2,112,3584]{2,1,0:T(8,128)}, u32[]{:S(2)}) copy-start(f32[2,112,3584]{2,1,0:T(8,128)} %param.17) | copy-start | bytes 9633796
  881.8 10.9 %copy-start.11 = (bf16[1,112,3584]{2,1,0:T(8,128)(2,1)S(1)}, bf16[1,112,3584]{2,1,0:T(8,128)(2,1)}, u32[]{:S(2)}) copy-start(bf16[1,112,3584]{2,1,0:T(8,128)(2,1)} %get-tuple-element.9) | copy-start | bytes 2408452
  881.8 11.1 %copy-start.12 = (bf16[1,112,3584]{2,1,0:T(8,128)(2,1)S(1)}, bf16[1,112,3584]{2,1,0:T(8,128)(2,1)}, u32[]{:S(2)}) copy-start(bf16[1,112,3584]{2,1,0:T(8,128)(2,1)} %get-tuple-element.10) | copy-start | bytes 2408452
Sparse Core Ops, SparseCore 0:
  10.4 47.8 all-gather.12
  60.7 43.8 all-gather.14
  107.0 43.8 all-gather.16
  153.2 43.8 all-gather.20
  199.4 43.8 all-gather.22
  245.6 43.8 all-gather.18
  399.4 45.0 reduce-scatter.14
  447.0 45.3 reduce-scatter.16
  495.1 45.3 reduce-scatter.10
  542.9 45.3 reduce-scatter.12
  590.9 45.3 reduce-scatter.6
  638.8 45.3 reduce-scatter.8
  688.5 167.3 all-reduce.2
where the time goes:
time: 916 us; the launch traced here: 908 us
  waiting for transfers between devices  441 us (48%)
  matrix products  380 us (41%)
  other arithmetic  30 us (3%)
  local copies, waits for them, and re-layouts  25.4 us (3%)
  between operations  17 us (2%)
  blocking collectives  14.6 us (2%)
    psum x1, waiting for transfers between devices, summed(): lax.psum(lax.psum_scatter(term, 's', scatter_dimension=0, tiled=True), 'r')  172 us
    dot_general x5, matrix products, layer(): gate = jnp.dot(a, w['w_gate'], preferred_element_type=jnp.float32)  140 us
    reduce_scatter x6, waiting for transfers between devices, summed(): lax.psum_scatter(term, 's', scatter_dimension=0, tiled=True)  134 us
    all_gather x6, waiting for transfers between devices, fetched(): lax.all_gather(w[number], 's', axis=0, tiled=True)  133 us
    dot_general x5, matrix products, layer(): up = jnp.dot(a, w['w_up'], preferred_element_type=jnp.float32)  129 us
    dot_general x5, matrix products, matmul(): jnp.dot(a, w, preferred_element_type=jnp.float32).astype(jnp.bfloat16)  111 us
    unnamed x42, local copies, waits for them, and re-layouts  18.7 us
  transfers between devices with their start and end apart: 13, of which 10 were waited for; matrix products, arithmetic and copies ran while one was open for 32% of the time, Pallas kernels for 0%

commit v1 on v0

v1 whole, which is shorter than its diff:
```python
import functools

import jax
import jax.numpy as jnp
from jax import lax
from jax.experimental import pallas as pl
from jax.experimental.pallas import tpu as pltpu
from jax.sharding import PartitionSpec as P

NX, NC, NY = 4, 2, 4
S = NX * NC
U = 512
UB = U // S
LANES = 128
F32, BF16 = jnp.float32, jnp.bfloat16
MESH = pl.DeviceIdType.MESH
EPS = 1e-6


def nn(a, b):
    return lax.dot_general(a, b, (((1,), (0,)), ((), ())), preferred_element_type=F32)


def nt(a, b):
    return lax.dot_general(a, b, (((1,), (1,)), ((), ())), preferred_element_type=F32)


def tn(a, b):
    return lax.dot_general(a, b, (((0,), (0,)), ((), ())), preferred_element_type=F32)


def normed(h):
    wide = h.astype(F32)
    scale = lax.rsqrt(jnp.mean(wide * wide, -1, keepdims=True) + EPS)
    return (wide * scale).astype(BF16)


def glu_backward(g, u, dh):
    sig = jax.nn.sigmoid(g)
    silu = g * sig
    by_silu = dh * u
    return (silu * u).astype(BF16), (by_silu * (sig + silu * (1.0 - sig))).astype(BF16), (silu * dh).astype(BF16)


class Copy:
    def __init__(self, **what):
        self.what = what

    def __getattr__(self, name):
        return getattr(pltpu.make_async_remote_copy(**self.what), name)


def prep_kernel(wg, wu, og, ou, *, n_units):
    low = lax.broadcasted_iota(jnp.int32, (wg.shape[1], LANES), 1) < UB
    for w, o in ((wg, og), (wu, ou)):
        for j in range(n_units):
            for a in range(S // 2):
                first = (2 * a + j % 2) * n_units + j
                second = (2 * a + 1 - j % 2) * n_units + j
                one = w[0, :, pl.ds(first // 2 * LANES, LANES)]
                two = w[0, :, pl.ds(second // 2 * LANES, LANES)]
                o[0, j, :, pl.ds(a * LANES, LANES)] = jnp.where(low, one, two)


def prep(w_gate, w_up):
    layers, rows, ff = w_gate.shape
    n_units = ff // U
    out = jax.ShapeDtypeStruct((layers, n_units, rows, U), BF16)
    return pl.pallas_call(
        functools.partial(prep_kernel, n_units=n_units),
        grid=(layers,),
        in_specs=[pl.BlockSpec((1, rows, ff), lambda l: (l, 0, 0))] * 2,
        out_specs=[pl.BlockSpec((1, n_units, rows, U), lambda l: (l, 0, 0, 0))] * 2,
        out_shape=[out, out],
        name="prep",
    )(w_gate, w_up)


def forward_kernel(x, wg, wu, wd, h1, aT, gate, up, a, acc, *, tile):
    j = pl.program_id(0)
    tokens, d = x.shape

    @pl.when(j == 0)
    def _():
        def norm(r, _):
            rows = pl.ds(pl.multiple_of(r * tile, tile), tile)
            wide = x[rows].astype(F32)
            scale = lax.rsqrt(jnp.mean(wide * wide, -1, keepdims=True) + EPS)
            wide = wide * scale
            a[rows] = wide.astype(BF16)
            aT[:, rows] = wide.T.astype(BF16)
            acc[rows] = jnp.zeros((tile, d), F32)
            return 0

        lax.fori_loop(0, tokens // tile, norm, 0)

    swap = lax.rem(j, 2)
    w_g = wg[:, 0].reshape(d, U)
    w_u = wu[:, 0].reshape(d, U)
    w_d = jnp.concatenate([wd[2 * i + (q + swap - 2 * q * swap), 0] for i in range(S // 2) for q in range(2)], axis=0)
    for r in range(tokens // tile):
        rows = pl.ds(r * tile, tile)
        g = nn(a[rows], w_g)
        u = nn(a[rows], w_u)
        gate[0, rows] = g
        up[0, rows] = u
        hid = (g * jax.nn.sigmoid(g) * u).astype(BF16)
        acc[rows] += nn(hid, w_d)

    @pl.when(j == pl.num_programs(0) - 1)
    def _():
        def finish(r, _):
            rows = pl.ds(pl.multiple_of(r * tile, tile), tile)
            h1[rows] = x[rows] + acc[rows].astype(BF16)
            return 0

        lax.fori_loop(0, tokens // tile, finish, 0)


def forward(x, wg, wu, wd):
    tokens, d = x.shape
    n_units = wg.shape[1]
    tile = min(512, tokens)
    once = pl.Buffered(1)
    const = lambda shape: pl.BlockSpec(shape, lambda j: (0, 0), pipeline_mode=once)
    return pl.pallas_call(
        functools.partial(forward_kernel, tile=tile),
        grid=(n_units,),
        in_specs=[
            const((tokens, d)),
            pl.BlockSpec((S, 1, d // S, U), lambda j: (0, j, 0, 0)),
            pl.BlockSpec((S, 1, d // S, U), lambda j: (0, j, 0, 0)),
            pl.BlockSpec((S, 1, UB, d), lambda j: (0, j, 0, 0)),
        ],
        out_specs=[
            const((tokens, d)),
            const((d, tokens)),
            pl.BlockSpec((1, tokens, U), lambda j: (j, 0, 0)),
            pl.BlockSpec((1, tokens, U), lambda j: (j, 0, 0)),
        ],
        out_shape=[
            jax.ShapeDtypeStruct((tokens, d), BF16),
            jax.ShapeDtypeStruct((d, tokens), BF16),
            jax.ShapeDtypeStruct((n_units, tokens, U), F32),
            jax.ShapeDtypeStruct((n_units, tokens, U), F32),
        ],
        scratch_shapes=[pltpu.VMEM((tokens, d), BF16), pltpu.VMEM((tokens, d), F32)],
        compiler_params=pltpu.CompilerParams(vmem_limit_bytes=62 * 2**20),
        cost_estimate=pl.CostEstimate(flops=6 * tokens * d * U * n_units, bytes_accessed=tokens * U * n_units * 8, transcendentals=0),
        name="forward",
    )(x, wg, wu, wd)


def backward_kernel(
    h1, dy, a0T, gate0, up0, wg1, wu1, wd1, wd0,
    fgu, fd, ss,
    a1, aT, dyv, acc, hid, dgt, dup, wgv, wuv, wdv,
    ggu, gd, pgu, pd,
    sa1, ra1, sb1, rb1, sa2, ra2, sb2, rb2, res1, res2,
    sa3, ra3, sb3, rb3, sa4, ra4, sb4, rb4, q1, q2,
    zs1, zs2, zr1, zr2, gz1, gz2,
    wsem, asem, tsem,
    psend, precv, s1s, s1r, s2s, s2r, s3s, s3r, s4s, s4r, zss, zsr, gss, gsr, gls, ys, yr,
    *, tile, nz,
):
    tokens, d = dyv.shape
    units = wg1.shape[1]
    n_tiles = tokens // tile
    ngz = nz - 1
    half = ngz - ngz // 2

    s, r = lax.axis_index("s"), lax.axis_index("r")
    x, c = lax.div(s, 2), lax.rem(s, 2)
    y, z = lax.div(r, nz), lax.rem(r, nz)
    turn = lambda i, by, n: lax.rem(i + by + n, n)
    x_dev = lambda k: {"s": turn(x, k, NX) * 2 + c}
    y_dev = lambda k: {"r": turn(y, k, NY) * nz + z}
    z_dev = lambda k: {"r": y * nz + k}
    partner = {"s": x * 2 + 1 - c}

    def remote(src, dst, send, recv, dev):
        return Copy(src_ref=src, dst_ref=dst, send_sem=send, recv_sem=recv, device_id=dev, device_id_type=MESH)

    barrier = pltpu.get_barrier_semaphore()
    peers = [partner, x_dev(1), x_dev(-1), y_dev(1), y_dev(-1)]
    peers += [z_dev(turn(z, k, nz)) for k in range(1, nz)]
    for dev in peers:
        pl.semaphore_signal(barrier, inc=1, device_id=dev, device_id_type=MESH)
    pl.semaphore_wait(barrier, len(peers))


    class Ring:
        def __init__(self, me, dev, get, put, sa, ra, sb, rb, send, recv, slot_a, slot_b):
            self.me, self.get, self.put = me, get, put
            self.a = [
                remote(sa[0], ra[0], send.at[0], recv.at[slot_b, 0], dev(1)),
                remote(sa[1], ra[1], send.at[1], recv.at[slot_b, 1], dev(-1)),
            ]
            self.b = [[remote(sb[w][h], rb[w][h], send.at[2 + 2 * w + h], recv.at[slot_b, 2 + 2 * w + h], dev(1 - 2 * w)) for h in range(2)] for w in range(2)]
            self.sa, self.ra, self.sb, self.rb = sa, ra, sb, rb

        def start(self):
            far = turn(self.me, 2, 4)
            for h in range(2):
                self.sa[h][...] = self.get(far, h).astype(BF16)
                self.a[h].start()
            self.sb[0][1][...] = self.get(turn(self.me, 1, 4), 1).astype(BF16)
            self.b[0][1].start()
            self.sb[1][0][...] = self.get(turn(self.me, -1, 4), 0).astype(BF16)
            self.b[1][0].start()

        def middle(self):
            for h in range(2):
                self.a[h].wait_recv()
                near = turn(self.me, 1 - 2 * h, 4)
                self.sb[h][h][...] = (self.get(near, h) + self.ra[h][...].astype(F32)).astype(BF16)
                self.b[h][h].start()
            for h in range(2):
                self.a[h].wait_send()

        def end(self):
            for w in range(2):
                for h in range(2):
                    self.b[w][h].wait_recv()
            for h in range(2):
                self.put(h, self.get(self.me, h) + self.rb[0][h][...].astype(F32) + self.rb[1][h][...].astype(F32))
            for w in range(2):
                for h in range(2):
                    self.b[w][h].wait_send()

    def flip(u):
        j = jnp.where(u >= units, u - units, u)
        return lax.rem(j, 2)

    def ring1(u):
        g, p, a2 = lax.rem(u, 2), lax.rem(u, 3), lax.rem(u, 2)

        def get(k, h):
            return ggu[g, h, k, c].astype(F32) + pgu[p, h, k].astype(F32)

        def put(h, total):
            for k in range(NY):
                res1[k, h] = total[:, k * LANES : (k + 1) * LANES]

        return Ring(x, x_dev, get, put, [sa1.at[h] for h in range(2)], [ra1.at[a2, h] for h in range(2)],
                    [[sb1.at[a2, w, h] for h in range(2)] for w in range(2)], [[rb1.at[p, w, h] for h in range(2)] for w in range(2)], s1s.at[a2], s1r, a2, p)

    def ring2(u):
        g, p, a2 = lax.rem(u, 2), lax.rem(u, 3), lax.rem(u, 2)
        f = flip(u)
        pos = c + f - 2 * c * f

        def get(k, h):
            return gd[g, 2 * h : 2 * h + 2, pos, k].astype(F32) + pd[p, 2 * h : 2 * h + 2, k].astype(F32)

        def put(h, total):
            res2[2 * h : 2 * h + 2] = total

        return Ring(y, y_dev, get, put, [sa2.at[h] for h in range(2)], [ra2.at[a2, h] for h in range(2)],
                    [[sb2.at[a2, w, h] for h in range(2)] for w in range(2)], [[rb2.at[p, w, h] for h in range(2)] for w in range(2)], s2s.at[a2], s2r, a2, p)

    def ring3(u):
        a2 = lax.rem(u, 2)

        def get(k, h):
            return res1[k, h]

        def put(h, total):
            rows = total.shape[0] // ngz
            for k in range(ngz):
                q1[k, h] = total[k * rows : (k + 1) * rows]

        return Ring(y, y_dev, get, put, [sa3.at[h] for h in range(2)], [ra3.at[a2, h] for h in range(2)],
                    [[sb3.at[w, h] for h in range(2)] for w in range(2)], [[rb3.at[a2, w, h] for h in range(2)] for w in range(2)], s3s, s3r, a2, a2)

    cut = [slice(0, 512), slice(512, d)]

    def ring4(u):
        a2 = lax.rem(u, 2)

        def get(k, h):
            return res2[k, :, cut[h]]

        def put(h, total):
            q2[:, cut[h]] = total

        return Ring(x, x_dev, get, put, [sa4.at[:, cut[h]] for h in range(2)], [ra4.at[a2, :, cut[h]] for h in range(2)],
                    [[sb4.at[w, :, cut[h]] for h in range(2)] for w in range(2)], [[rb4.at[a2, w, :, cut[h]] for h in range(2)] for w in range(2)], s4s, s4r, a2, a2)


    def to_partner(u):
        g, p, f = lax.rem(u, 2), lax.rem(u, 3), flip(u)
        other = 1 - c
        pos = other + f - 2 * other * f
        return [
            remote(ggu.at[g, 0, :, other], pgu.at[p, 0], psend.at[0], precv.at[p, 0], partner),
            remote(ggu.at[g, 1, :, other], pgu.at[p, 1], psend.at[1], precv.at[p, 1], partner),
            remote(gd.at[g, :, pos], pd.at[p], psend.at[2], precv.at[p, 2], partner),
        ]

    def c1(u):
        copies = to_partner(u)
        copies[0].wait_recv()
        copies[1].wait_recv()
        ring1(u).start()
        copies[2].wait_recv()
        ring2(u).start()
        for copy in copies:
            copy.wait_send()

    def c2(u):
        ring1(u).middle()
        ring2(u).middle()

    def c3(u):
        ring1(u).end()
        ring3(u).start()
        ring2(u).end()
        ring4(u).start()

    def c4(u):
        ring3(u).middle()
        ring4(u).middle()

    def z_copies(u, k):
        a2 = lax.rem(u, 2)
        return [
            remote(zs1.at[k], zr1.at[a2, z], zss.at[k, 0], zsr.at[a2, z, 0], z_dev(k)),
            remote(zs2.at[k], zr2.at[a2, z], zss.at[k, 1], zsr.at[a2, z, 1], z_dev(k)),
        ]

    def c5(u):
        ring3(u).end()
        ring4(u).end()
        cols = d // ngz
        for k in range(ngz):
            zs1[k] = q1[k].astype(BF16)
            zs2[k] = q2[:, k * cols : (k + 1) * cols].astype(BF16)

            @pl.when(k != z)
            def _():
                for copy in z_copies(u, k):
                    copy.start()

    def gather_copies(u, k):
        a2 = lax.rem(u, 2)
        return [
            remote(gz1, fgu.at[u, y, z], gss.at[k, 0], gsr.at[a2, z, 0], z_dev(k)),
            remote(gz2, fd.at[u, y, z], gss.at[k, 1], gsr.at[a2, z, 1], z_dev(k)),
        ]

    def own_copies(u):
        return [pltpu.make_async_copy(gz1, fgu.at[u, y, z], gls.at[0]), pltpu.make_async_copy(gz2, fd.at[u, y, z], gls.at[1])]

    def c6(u):
        a2 = lax.rem(u, 2)

        @pl.when(z < ngz)
        def _():
            one, two = jnp.zeros(gz1.shape, F32), jnp.zeros(gz2.shape, F32)
            for k in range(nz):

                @pl.when(k != z)
                def _():
                    remote(zs1.at[0], zr1.at[a2, k], zss.at[0, 0], zsr.at[a2, k, 0], z_dev(z)).wait_recv()
                    remote(zs2.at[0], zr2.at[a2, k], zss.at[0, 1], zsr.at[a2, k, 1], z_dev(z)).wait_recv()

                own = k == z
                zone = lax.rem(z, ngz)
                one += jnp.where(own, q1[zone], zr1[a2, k].astype(F32))
                two += jnp.where(own, q2[:, pl.ds(pl.multiple_of(zone * (d // ngz), LANES), d // ngz)], zr2[a2, k].astype(F32))
            one, two = one.astype(BF16), two.astype(BF16)
            gz1[...], gz2[...] = one, two
            one, two = one.astype(F32), two.astype(F32)
            ss[...] += jnp.full(ss.shape, jnp.sum(one * one) + jnp.sum(two * two))
            for copy in own_copies(u):
                copy.start()
            for k in range(nz):

                @pl.when(k != z)
                def _():
                    for copy in gather_copies(u, k):
                        copy.start()

        for k in range(ngz):

            @pl.when(k != z)
            def _():
                for copy in z_copies(u, k):
                    copy.wait_send()

    def y_copies(u, by):
        a2 = lax.rem(u, 2)
        w = 0 if by > 0 else 1
        k = turn(y, -by, NY)
        fds = [slice(0, half), slice(half, ngz)][w]
        return [
            remote(fgu.at[u, y], fgu.at[u, y], ys.at[w, 0], yr.at[a2, w, 0], y_dev(by)),
            remote(fd.at[u, y], fd.at[u, y], ys.at[w, 1], yr.at[a2, w, 1], y_dev(by)),
        ], [
            remote(fgu.at[u, k, :, w], fgu.at[u, k, :, w], ys.at[w, 2], yr.at[a2, w, 2], y_dev(by)),
            remote(fd.at[u, k, fds], fd.at[u, k, fds], ys.at[w, 3], yr.at[a2, w, 3], y_dev(by)),
        ]

    def c7(u):
        a2 = lax.rem(u, 2)
        for k in range(ngz):

            @pl.when(k != z)
            def _():
                remote(gz1, fgu.at[u, y, k], gss.at[0, 0], gsr.at[a2, k, 0], z_dev(z)).wait_recv()
                remote(gz2, fd.at[u, y, k], gss.at[0, 1], gsr.at[a2, k, 1], z_dev(z)).wait_recv()

        @pl.when(z < ngz)
        def _():
            for copy in own_copies(u):
                copy.wait()
            for k in range(nz):

                @pl.when(k != z)
                def _():
                    for copy in gather_copies(u, k):
                        copy.wait_send()

        for by in (1, -1):
            for copy in y_copies(u, by)[0]:
                copy.start()

    def incoming(u, by, copies):
        a2 = lax.rem(u, 2)
        w = 0 if by > 0 else 1
        near, far = turn(y, -by, NY), turn(y, -2 * by, NY)
        fds = [slice(0, half), slice(half, ngz)][w]
        if copies == 0:
            return [
                remote(fgu.at[u, y], fgu.at[u, near], ys.at[w, 0], yr.at[a2, w, 0], y_dev(by)),
                remote(fd.at[u, y], fd.at[u, near], ys.at[w, 1], yr.at[a2, w, 1], y_dev(by)),
            ]
        return [
            remote(fgu.at[u, y, :, w], fgu.at[u, far, :, w], ys.at[w, 2], yr.at[a2, w, 2], y_dev(by)),
            remote(fd.at[u, y, fds], fd.at[u, far, fds], ys.at[w, 3], yr.at[a2, w, 3], y_dev(by)),
        ]

    def c8(u):
        for by in (1, -1):
            for copy in incoming(u, by, 0):
                copy.wait_recv()
            for copy in y_copies(u, by)[1]:
                copy.start()

    def c9(u):
        for by in (1, -1):
            for copy in incoming(u, by, 1):
                copy.wait_recv()
            for group in y_copies(u, by):
                for copy in group:
                    copy.wait_send()

    plan = {0: ((c5, 3), (c7, 4)), 1: ((c1, 1),), 2: ((c3, 2), (c8, 4)), 3: ((c6, 3), (c4, 2)), 4: ((c2, 1), (c9, 4))}

    def steps(t, place):
        for step, behind in plan[place]:
            u = t - behind

            @pl.when((u >= 0) & (u < 2 * units))
            def _():
                step(u)


    def weights(j, layer1):
        swap = lax.rem(j, 2)
        copies = []
        if layer1:
            copies += [pltpu.make_async_copy(wg1.at[:, j], wgv, wsem.at[0]), pltpu.make_async_copy(wu1.at[:, j], wuv, wsem.at[1])]
        wd = wd1 if layer1 else wd0
        for q in range(2):
            copies.append(pltpu.make_async_copy(wd.at[:, q, j], wdv.at[:, q + swap - 2 * q * swap], wsem.at[2 + q]))
        return copies

    def weight_gradients(t):
        g = lax.rem(t, 2)
        copies = to_partner(t)
        ggu[g, 0] = nn(aT[...], dgt[...]).astype(BF16).reshape(ggu.shape[2:])
        copies[0].start()
        steps(t, 3)
        ggu[g, 1] = nn(aT[...], dup[...]).astype(BF16).reshape(ggu.shape[2:])
        copies[1].start()
        steps(t, 4)
        gd[g] = tn(hid[...], dyv[...]).astype(BF16).reshape(gd.shape[1:])
        copies[2].start()

    first = weights(0, True)
    for copy in first:
        copy.start()
    loads = [pltpu.make_async_copy(h1, a1, asem.at[0]), pltpu.make_async_copy(dy, dyv, asem.at[1])]
    for copy in loads:
        copy.start()
    ss[...] = jnp.zeros(ss.shape, F32)
    for copy in loads:
        copy.wait()

    def norm(i, _):
        rows = pl.ds(pl.multiple_of(i * tile, tile), tile)
        wide = a1[rows].astype(F32)
        scale = lax.rsqrt(jnp.mean(wide * wide, -1, keepdims=True) + EPS)
        wide = wide * scale
        a1[rows] = wide.astype(BF16)
        aT[:, rows] = wide.T.astype(BF16)
        acc[0, rows] = jnp.zeros((tile, d), F32)
        acc[1, rows] = jnp.zeros((tile, d), F32)
        return 0

    lax.fori_loop(0, n_tiles, norm, 0)

    def both_passes(t, _):
        steps(t, 0)
        for copy in weights(t, True):
            copy.wait()
        w_g, w_u = wgv[...].reshape(d, U), wuv[...].reshape(d, U)
        w_d = wdv[...].reshape(U, d)
        for i in range(n_tiles):
            rows = pl.ds(i * tile, tile)
            av = a1[rows]
            g, u = nn(av, w_g), nn(av, w_u)
            dh = nt(dyv[rows], w_d).astype(BF16).astype(F32)
            one, by_gate, by_up = glu_backward(g, u, dh)
            hid[rows], dgt[rows], dup[rows] = one, by_gate, by_up
            acc[0, rows] += nt(by_up, w_u)
            acc[1, rows] += nt(by_gate, w_g)
            if i == min(1, n_tiles - 1):
                steps(t, 1)
        steps(t, 2)

        @pl.when(t < units - 1)
        def _():
            for copy in weights(t + 1, True):
                copy.start()

        @pl.when(t == units - 1)
        def _():
            for copy in weights(0, False):
                copy.start()

        weight_gradients(t)
        return 0

    lax.fori_loop(0, units, both_passes, 0)

    load = pltpu.make_async_copy(h1, a1, asem.at[0])
    load.start()
    loadT = pltpu.make_async_copy(a0T, aT, asem.at[1])
    loadT.start()
    load.wait()

    def cotangent(i, _):
        rows = pl.ds(pl.multiple_of(i * tile, tile), tile)
        wide = a1[rows].astype(F32)
        scale = lax.rsqrt(jnp.mean(wide * wide, -1, keepdims=True) + EPS)
        by_a = (acc[0, rows].astype(BF16).astype(F32) + acc[1, rows].astype(BF16).astype(F32)).astype(BF16).astype(F32)
        inner = jnp.sum(wide * by_a, -1, keepdims=True)
        by_h = by_a * scale - wide * (inner * (scale * scale * scale) * (1.0 / d))
        dyv[rows] = (dyv[rows].astype(F32) + by_h.astype(BF16).astype(F32)).astype(BF16)
        return 0

    lax.fori_loop(0, n_tiles, cotangent, 0)
    loadT.wait()

    def tiles(j, i, slot):
        rows = pl.ds(i * tile, tile)
        here = pl.ds(slot * tile, tile)
        return [
            pltpu.make_async_copy(gate0.at[j, rows], acc.at[0, here, 0:U], tsem.at[slot, 0]),
            pltpu.make_async_copy(up0.at[j, rows], acc.at[1, here, 0:U], tsem.at[slot, 1]),
        ]

    for i in range(n_tiles):
        for copy in tiles(0, i, i):
            copy.start()

    def backward_only(t, _):
        j = t - units
        steps(t, 0)
        for copy in weights(j, False):
            copy.wait()
        w_d = wdv[...].reshape(U, d)
        for i in range(n_tiles):
            rows = pl.ds(i * tile, tile)
            for copy in tiles(j, i, i):
                copy.wait()
            dh = nt(dyv[rows], w_d).astype(BF16).astype(F32)
            hid[rows], dgt[rows], dup[rows] = glu_backward(acc[0, rows, 0:U], acc[1, rows, 0:U], dh)
            if i == min(1, n_tiles - 1):
                steps(t, 1)
        steps(t, 2)

        @pl.when(j < units - 1)
        def _():
            for copy in weights(j + 1, False):
                copy.start()
            for i in range(n_tiles):
                for copy in tiles(j + 1, i, i):
                    copy.start()

        weight_gradients(t)
        return 0

    lax.fori_loop(units, 2 * units, backward_only, 0)

    def drain(t, _):
        for place in range(5):
            steps(t, place)
        return 0

    lax.fori_loop(2 * units, 2 * units + 5, drain, 0)


def backward(h1, dy, a0T, gate0, up0, wg1, wu1, wd1, wd0, nz):
    tokens, d = h1.shape
    units = wg1.shape[1]
    tile = min(512, tokens)
    rg, ngz = d // S, nz - 1
    rz, cz, rd = rg // ngz, d // ngz, UB // NY
    wd1, wd0 = (w.reshape(NX, NC, units, UB, d) for w in (wd1, wd0))
    vmem = lambda *shape, dtype=BF16: pltpu.VMEM(shape, dtype)
    dma = lambda *shape: pltpu.SemaphoreType.DMA(shape)
    scratch = [
        vmem(tokens, d), vmem(d, tokens), vmem(tokens, d), vmem(2, tokens, d, dtype=F32),
        vmem(tokens, U), vmem(tokens, U), vmem(tokens, U),
        vmem(S, rg, U), vmem(S, rg, U), vmem(NX, NC, UB, d),
        vmem(2, 2, NX, NC, rg, U), vmem(2, NX, NC, NY, rd, d), vmem(3, 2, NX, rg, U), vmem(3, NX, NY, rd, d),
        vmem(2, rg, U), vmem(2, 2, rg, U), vmem(2, 2, 2, rg, U), vmem(3, 2, 2, rg, U),
        vmem(2, 2, rd, d), vmem(2, 2, 2, rd, d), vmem(2, 2, 2, 2, rd, d), vmem(3, 2, 2, 2, rd, d),
        vmem(NY, 2, rg, LANES, dtype=F32), vmem(NX, rd, d, dtype=F32),
        vmem(2, rg, LANES), vmem(2, 2, rg, LANES), vmem(2, 2, rg, LANES), vmem(2, 2, 2, rg, LANES),
        vmem(rd, d), vmem(2, rd, d), vmem(2, rd, d), vmem(2, 2, rd, d),
        vmem(ngz, 2, rz, LANES, dtype=F32), vmem(rd, d, dtype=F32),
        vmem(ngz, 2, rz, LANES), vmem(ngz, rd, cz), vmem(2, nz, 2, rz, LANES), vmem(2, nz, rd, cz),
        vmem(2, rz, LANES), vmem(rd, cz),
        dma(4), dma(2), dma(max(1, tokens // tile), 2),
        dma(3), dma(3, 3), dma(2, 6), dma(3, 6), dma(2, 6), dma(3, 6), dma(6), dma(2, 6), dma(6), dma(2, 6),
        dma(ngz, 2), dma(2, nz, 2), dma(nz, 2), dma(2, nz, 2), dma(2), dma(2, 4), dma(2, 2, 4),
    ]
    anywhere = pl.BlockSpec(memory_space=pl.ANY)
    return pl.pallas_call(
        functools.partial(backward_kernel, tile=tile, nz=nz),
        in_specs=[anywhere] * 9,
        out_specs=[anywhere, anywhere, pl.BlockSpec(memory_space=pltpu.VMEM)],
        out_shape=[
            jax.ShapeDtypeStruct((2 * units, NY, ngz, 2, rz, LANES), BF16),
            jax.ShapeDtypeStruct((2 * units, NY, ngz, rd, cz), BF16),
            jax.ShapeDtypeStruct((8, LANES), F32),
        ],
        scratch_shapes=scratch,
        compiler_params=pltpu.CompilerParams(collective_id=1, has_side_effects=True, vmem_limit_bytes=67043328),
        cost_estimate=pl.CostEstimate(flops=24 * tokens * d * U * units, bytes_accessed=2**26, transcendentals=0),
        name="backward",
    )(h1, dy, a0T, gate0, up0, wg1, wu1, wd1, wd0)


def step_kernel(factor, fgu, fd, wg, mg, vg, wu, mu, vu, wd, md, vd, *out, n_units):
    ngz, rd, cz = fd.shape[2:]
    fac = factor[0, 0]

    def adamw(g, w, m, v, outs):
        g = g.astype(F32) * fac
        m = 0.9 * m + 0.1 * g
        v = 0.95 * v + 0.05 * g * g
        step = m * lax.rsqrt(v + 1e-8) + 0.1 * w.astype(F32)
        return (w.astype(F32) - 0.02 * step).astype(BF16), m, v

    rows = wg.shape[1]
    low = lax.broadcasted_iota(jnp.int32, (rows, LANES), 1) < UB
    for h, (w, m, v, outs) in enumerate(((wg, mg, vg, out[0::3]), (wu, mu, vu, out[1::3]))):
        by_unit = [jnp.concatenate([fgu[j, 0, k, h] for k in range(ngz)], axis=0).astype(F32) for j in range(n_units)]
        for i in range(n_units):
            at = pl.ds(i * LANES, LANES)
            g = jnp.where(low, by_unit[2 * i % n_units], by_unit[(2 * i + 1) % n_units])
            outs[0][0, :, at], outs[1][0, :, at], outs[2][0, :, at] = adamw(g, w[0, :, at], m[0, :, at], v[0, :, at], outs)
    for j in range(n_units):
        g = jnp.concatenate([fd[j, 0, k] for k in range(ngz)], axis=1)
        outs = out[2::3]
        outs[0][0, j, 0], outs[1][0, j, 0], outs[2][0, j, 0] = adamw(g, wd[0, j, 0], md[0, j, 0], vd[0, j, 0], outs)


def optimizer(factor, fgu, fd, weights, m, v):
    layers, rg, ff = weights[0].shape
    n_units = ff // U
    d = weights[2].shape[2]
    _, _, ngz, rd, cz = fd.shape
    rz = rg // ngz
    wide = ff // NY
    down = lambda a: a.reshape(layers, n_units, NY, rd, d)
    col = pl.BlockSpec((1, rg, wide), lambda l, a: (l, 0, a))
    row = pl.BlockSpec((1, n_units, 1, rd, d), lambda l, a: (l, 0, a, 0, 0))
    args = []
    for i in range(3):
        args += [w if i < 2 else down(w) for w in (weights[i], m[i], v[i])]
    shapes = lambda dtype: [jax.ShapeDtypeStruct((layers, rg, ff), dtype)] * 2 + [jax.ShapeDtypeStruct((layers, n_units, NY, rd, d), dtype)]
    out = pl.pallas_call(
        functools.partial(step_kernel, n_units=n_units),
        grid=(layers, NY),
        in_specs=[
            pl.BlockSpec(memory_space=pltpu.SMEM),
            pl.BlockSpec((n_units, 1, ngz, 2, rz, LANES), lambda l, a: (1 - l, a, 0, 0, 0, 0)),
            pl.BlockSpec((n_units, 1, ngz, rd, cz), lambda l, a: (1 - l, a, 0, 0, 0)),
        ]
        + [col] * 6
        + [row] * 3,
        out_specs=[col, col, row] * 3,
        out_shape=shapes(BF16) + shapes(F32) + shapes(F32),
        name="adamw",
    )(factor, fgu, fd, *args)
    return tuple(o.reshape(layers, -1, d) if i % 3 == 2 else o for i, o in enumerate(out))


def solution(mesh):
    nz = mesh.shape["r"] // NY

    def step(x, dy, *arrays):
        weights, m, v = (arrays[i : i + 3] for i in (0, 3, 6))
        layers, rg, ff = weights[0].shape
        n_units, d = ff // U, weights[2].shape[2]
        gates, ups = prep(weights[0], weights[1])
        downs = weights[2].reshape(layers, n_units, UB, d)
        whole = lambda w: lax.all_gather(w, "s", axis=0)
        wg, wu, wd = ([whole(w[l]) for l in range(layers)] for w in (gates, ups, downs))
        h1, a0T, gate0, up0 = forward(x[0], wg[0], wu[0], wd[0])
        fgu, fd, ss = backward(h1, dy[0], a0T, gate0, up0, wg[1], wu[1], wd[1], wd[0], nz)
        squares = lax.psum(ss[0, 0], ("r", "s"))
        count = lax.psum(1, "s") * sum(w.size for w in weights)
        factor = jnp.minimum(1.0, 0.5 * lax.rsqrt(squares / count + 1e-30))
        return optimizer(factor.reshape(1, 1), fgu, fd, weights, m, v)

    states, cut = P(("rep", "r", "s"), None, None), P(None, "s", None)
    return jax.shard_map(
        step,
        mesh=mesh,
        in_specs=(states, states) + (cut,) * 9,
        out_specs=(P("rep", "s", None),) * 9,
        check_vma=False,
    )
```

time: 916 us -> 694 us (0.76)
  matrix products: 380 us -> 0 us
  Pallas kernels: 0 us -> 376 us
  waiting for transfers between devices: 441 us -> 217 us
  blocking collectives: 14.6 us -> 78.9 us
  other arithmetic: 30 us -> 0 us
  local copies, waits for them, and re-layouts: 25.4 us -> 7.06 us
    dot_general x15 -> x0, matrix products: 380 us -> none  [the longest x5 140 us: layer(): gate = jnp.dot(a, w['w_gate'], preferred_element_type=jnp.float32)]
    pallas_call x0 -> x4, Pallas kernels: none -> 376 us  [the longest x1 294 us: backward(): pl.pallas_call(functools.partial(backward_kernel, tile=tile, nz=nz), in_s...]
    psum x1 -> x0, waiting for transfers between devices: 172 us -> none  [summed(): lax.psum(lax.psum_scatter(term, 's', scatter_dimension=0, tiled=True), 'r')]
    reduce_scatter x6 -> x0, waiting for transfers between devices: 134 us -> none  [summed(): lax.psum_scatter(term, 's', scatter_dimension=0, tiled=True)]
    all_gather x6, waiting for transfers between devices: 133 us -> 215 us  [step(): whole = lambda w: lax.all_gather(w, 's', axis=0)]
    psum x1, blocking collectives: 14.6 us -> 78.9 us  [step(): squares = lax.psum(ss[0, 0], ('r', 's'))]
    unnamed x42 -> x4, local copies, waits for them, and re-layouts: 18.7 us -> 0.59 us
    convert_element_type x2 -> x0, other arithmetic: 15.7 us -> none  [adamw(): return ((w - 0.02 * step).astype(jnp.bfloat16), m, v)]
  transfers between devices with their start and end apart: 13 -> 6, of which waited for: 10 -> 5; matrix products, arithmetic and copies ran while one was open for 32% -> 0% of each run, Pallas kernels for 0% -> 8%
where the time goes in v1:
time: 694 us
  Pallas kernels  376 us (54%)
  waiting for transfers between devices  217 us (31%)
  blocking collectives  78.9 us (11%)
  between operations  14.8 us (2%)
  local copies, waits for them, and re-layouts  7.06 us (1%)
    pallas_call x1, Pallas kernels, backward(): pl.pallas_call(functools.partial(backward_kernel, tile=tile, nz=nz), in_s...  294 us
    all_gather x6, waiting for transfers between devices, step(): whole = lambda w: lax.all_gather(w, 's', axis=0)  215 us
    psum x1, blocking collectives, step(): squares = lax.psum(ss[0, 0], ('r', 's'))  78.9 us
    pallas_call x1, Pallas kernels, forward(): pl.pallas_call(functools.partial(forward_kernel, tile=tile), grid=(n_unit...  58.9 us
    pallas_call x1, Pallas kernels, optimizer(): pl.pallas_call(functools.partial(step_kernel, n_units=n_units), grid=(lay...  20 us
  transfers between devices with their start and end apart: 6, of which 5 were waited for; matrix products, arithmetic and copies ran while one was open for 0% of the time, Pallas kernels for 8%

profile of v1, /device:TPU:1, one launch (start us, length us, event | category | flops | bytes accessed | tf_op | source)
XLA Modules:
  0.0 693.7 jit_solution(14695493937902442842)
XLA Ops:
  7.2 0.0 all-gather.7.cloned.1.call-start
  7.2 3.4 prep.1
  10.6 0.0 copy-start.1
  10.6 2.8 fusion.2
  13.4 0.0 copy-start
  13.4 0.0 all-gather.7.cloned.1.call-update
  13.4 0.0 all-gather.9.cloned.1.call-start
  13.4 0.0 copy-done.1
  13.4 1.3 fusion.1
  14.7 0.0 all-gather.9.cloned.1.call-update
  14.7 0.0 all-gather.11.cloned.1.call-start
  14.8 0.6 copy-done
  15.4 1.3 fusion
  16.6 0.0 all-gather.11.cloned.1.call-update
  16.7 0.0 all-gather.13.cloned.1.call-start
  16.7 0.5 all-gather.13.cloned.1.call-update
  17.2 0.0 all-gather.15.cloned.1.call-start
  17.3 0.5 all-gather.15.cloned.1.call-update
  17.8 0.0 all-gather.17.cloned.1.call-start
  17.9 0.5 all-gather.17.cloned.1.call-update
  18.4 43.0 %all-gather.7.cloned.1.call-done.wg = bf16[8,7,112,512]{3,2,1,0:T(8,128)(2,1)} async-done(((bf16[1,7,112,512]{3,2,1,0:T(8,128)(2,1)}), bf16[8,7,112,512]{3,2,1,0:T(8,128)(2,1)}) %all-gather.7.cloned.1.call-update) | async-done | bytes 6422544 | tf_op jit(solution)/shard_map/all_gather | solution.py:725
  61.4 46.3 %all-gather.9.cloned.1.call-done.wu = bf16[8,7,112,512]{3,2,1,0:T(8,128)(2,1)} async-done(((bf16[1,7,112,512]{3,2,1,0:T(8,128)(2,1)}), bf16[8,7,112,512]{3,2,1,0:T(8,128)(2,1)}) %all-gather.9.cloned.1.call-update) | async-done | bytes 6422544 | tf_op jit(solution)/shard_map/all_gather | solution.py:725
  107.7 46.3 %all-gather.11.cloned.1.call-done.wd = bf16[8,7,64,896]{3,2,1,0:T(8,128)(2,1)} async-done(((bf16[1,7,64,896]{3,2,1,0:T(8,128)(2,1)}), bf16[8,7,64,896]{3,2,1,0:T(8,128)(2,1)}) %all-gather.11.cloned.1.call-update) | async-done | bytes 6422544 | tf_op jit(solution)/shard_map/all_gather | solution.py:725
  154.0 58.9 %forward.1 = (bf16[2048,896]{1,0:T(8,128)(2,1)}, bf16[896,2048]{1,0:T(8,128)(2,1)}, f32[7,2048,512]{2,1,0:T(8,128)}, f32[7,2048,512]{2,1,0:T(8,128)}) custom-call(bf16[2048,896]{1,0:T(8,128)(2,1)} %bitcast.21, bf16[8,7,112,512]{3,2,1,0:T(8,128)(2,1)} %all-gather.7.cloned.1.call-done.wg, bf16[8,7,112,512]{3,2,1,0:T(8,128)(2,1)} %all-gather.9.cloned.1.call-done.wu, ...), custom_call_target="tpu_custom_call" | custom-call | flops 39460012032 | bytes 58720256 | tf_op jit(solution)/shard_map/forward/pallas_call | solution.py:126
  213.0 0.0 all-gather.13.cloned.1.call-done.wg1
  213.0 33.4 %all-gather.15.cloned.1.call-done.wu1 = bf16[8,7,112,512]{3,2,1,0:T(8,128)(2,1)} async-done(((bf16[1,7,112,512]{3,2,1,0:T(8,128)(2,1)}), bf16[8,7,112,512]{3,2,1,0:T(8,128)(2,1)}) %all-gather.15.cloned.1.call-update) | async-done | bytes 6422544 | tf_op jit(solution)/shard_map/all_gather | solution.py:725
  246.4 46.2 %all-gather.17.cloned.1.call-done = bf16[8,7,64,896]{3,2,1,0:T(8,128)(2,1)} async-done(((bf16[1,7,64,896]{3,2,1,0:T(8,128)(2,1)}), bf16[8,7,64,896]{3,2,1,0:T(8,128)(2,1)}) %all-gather.17.cloned.1.call-update) | async-done | bytes 6422544 | tf_op jit(solution)/shard_map/all_gather | solution.py:725
  292.6 293.5 %backward.1 = (bf16[14,4,7,2,16,128]{5,4,3,2,1,0:T(8,128)(2,1)}, bf16[14,4,7,16,128]{4,3,2,1,0:T(8,128)(2,1)}, f32[8,128]{1,0:T(8,128)}) custom-call(bf16[2048,896]{1,0:T(8,128)(2,1)} %get-tuple-element.29.h1, bf16[2048,896]{1,0:T(8,128)(2,1)} %bitcast.22, bf16[896,2048]{1,0:T(8,128)(2,1)} %get-tuple-element.30.a0T, ...), custom_call_target="tpu_custom_call" | custom-call | flops 157840048128 | bytes 67108864 | tf_op jit(solution)/shard_map/backward/pallas_call | solution.py:644
  586.1 1.2 slice.35
  587.3 78.9 %psum.7 = f32[]{:T(128)} all-reduce(f32[]{:T(128)} %bitcast.6), channel_id=1, replica_groups=mesh['rep'=1,'r'=32,'s'=8] {'r','s'}, use_global_device_ids=true, to_apply=%region_0.0 | all-reduce | flops 1 | bytes 8 | tf_op jit(solution)/shard_map/psum | solution.py:729
  666.8 20.0 %adamw.1 = (bf16[2,112,3584]{2,1,0:T(8,128)(2,1)}, bf16[2,112,3584]{2,1,0:T(8,128)(2,1)}, bf16[2,7,4,16,896]{4,3,2,1,0:T(8,128)(2,1)}, f32[2,112,3584]{2,1,0:T(8...) custom-call(f32[1,1]{1,0:T(1,128)} %bitcast.7.factor, ...), custom_call_target="tpu_custom_call" | custom-call | tf_op jit(solution)/shard_map/adamw/pallas_call | solution.py:699
Async XLA Ops:
  7.2 54.2 %all-gather.7.cloned.1.call-start = ((), (), s32[]{:S(2)}) async-start(), calls=%async_computation | async-start | bytes 7225344 | tf_op jit(solution)/shard_map/all_gather | solution.py:725
  10.6 2.8 copy-start.1
  13.4 2.0 copy-start
  13.4 94.3 %all-gather.9.cloned.1.call-start = ((), (), s32[]{:S(2)}) async-start(), calls=%async_computation.1 | async-start | bytes 7225344 | tf_op jit(solution)/shard_map/all_gather | solution.py:725
  14.7 139.3 %all-gather.11.cloned.1.call-start = ((), (), s32[]{:S(2)}) async-start(), calls=%async_computation.2 | async-start | bytes 7225344 | tf_op jit(solution)/shard_map/all_gather | solution.py:725
  16.7 196.3 %all-gather.13.cloned.1.call-start = ((), (), s32[]{:S(2)}) async-start(), calls=%async_computation.3 | async-start | bytes 7225344 | tf_op jit(solution)/shard_map/all_gather | solution.py:725
  17.2 229.2 %all-gather.15.cloned.1.call-start = ((), (), s32[]{:S(2)}) async-start(), calls=%async_computation.4 | async-start | bytes 7225344 | tf_op jit(solution)/shard_map/all_gather | solution.py:725
  17.8 274.7 %all-gather.17.cloned.1.call-start = ((), (), s32[]{:S(2)}) async-start(), calls=%async_computation.5 | async-start | bytes 7225344 | tf_op jit(solution)/shard_map/all_gather | solution.py:725
Sparse Core Ops, SparseCore 0:
  13.5 47.8 all-gather.6
  63.8 43.8 all-gather.8
  110.1 43.8 all-gather.10
  156.3 43.8 all-gather.12
  202.5 43.8 all-gather.14
  248.7 43.8 all-gather.16

commit v2 on v0

v2 whole, which is shorter than its diff:
```python
import functools

import jax
import jax.numpy as jnp
from jax import lax
from jax.experimental import pallas as pl
from jax.experimental.pallas import tpu as pltpu
from jax.sharding import PartitionSpec as P

NX, NC, NY = 4, 2, 4
S = NX * NC
U = 512
UB = U // S
LANES = 128
TILE = 512
TWO, THREE, FOUR, SIX = 2, 3, 4, 6
BOTH = (0, 1)
F32, BF16 = jnp.float32, jnp.bfloat16
MESH = pl.DeviceIdType.MESH
EPS = 1e-6


def nn(a, b):
    return lax.dot_general(a, b, (((1,), (0,)), ((), ())), preferred_element_type=F32)


def nt(a, b):
    return lax.dot_general(a, b, (((1,), (1,)), ((), ())), preferred_element_type=F32)


def tn(a, b):
    return lax.dot_general(a, b, (((0,), (0,)), ((), ())), preferred_element_type=F32)


def scale_of(wide):
    return lax.rsqrt(jnp.mean(wide * wide, -1, keepdims=True) + EPS)


def other(bit, by):
    return bit + by - TWO * bit * by


def glu_backward(g, u, dh):
    sig = jax.nn.sigmoid(g)
    silu = g * sig
    by_silu = dh * u
    return (silu * u).astype(BF16), (by_silu * (sig + silu * (1.0 - sig))).astype(BF16), (silu * dh).astype(BF16)


class Copy:
    def __init__(self, **what):
        self.what = what

    def __getattr__(self, name):
        return getattr(pltpu.make_async_remote_copy(**self.what), name)


def start(copies):
    for copy in copies:
        copy.start()


def arrived(copies):
    for copy in copies:
        copy.wait_recv()


def sent(copies):
    for copy in copies:
        copy.wait_send()


def done(copies):
    for copy in copies:
        copy.wait()


def prep_kernel(wg, wu, wd, wgu, wdn, block, sem, *, units):
    layers, rows, _ = wg.shape
    s = lax.axis_index("s")
    x, c = lax.div(s, NC), lax.rem(s, NC)
    low = lax.broadcasted_iota(jnp.int32, (rows, LANES), 1) < UB
    copies = []
    for l in range(layers):
        for j in range(units):
            copies.append(pltpu.make_async_copy(wd.at[l, j], wdn.at[l * units + j, x, c], sem.at[1, l, j]))
    start(copies)
    for l in range(layers):
        for j in range(units):
            for h, w in enumerate((wg, wu)):
                for a in range(NX):
                    swap = j % TWO
                    first = (TWO * a + swap) * units + j
                    second = (TWO * a + 1 - swap) * units + j
                    one = w[l, :, pl.ds(first // TWO * LANES, LANES)]
                    two = w[l, :, pl.ds(second // TWO * LANES, LANES)]
                    block[l, j, h, :, pl.ds(a * LANES, LANES)] = jnp.where(low, one, two)
            copy = pltpu.make_async_copy(block.at[l, j], wgu.at[l * units + j, :, x, c], sem.at[0, l, j])
            copy.start()
            copies.append(copy)
    done(copies)


def prep(w_gate, w_up, w_down):
    layers, rows, ff = w_gate.shape
    units, d = ff // U, w_down.shape[-1]
    anywhere = pl.BlockSpec(memory_space=pl.ANY)
    return pl.pallas_call(
        functools.partial(prep_kernel, units=units),
        in_specs=[pl.BlockSpec(memory_space=pltpu.VMEM)] * 3,
        out_specs=[anywhere] * 2,
        out_shape=[jax.ShapeDtypeStruct((layers * units, 2, NX, NC, rows, U), BF16), jax.ShapeDtypeStruct((layers * units, NX, NC, UB, d), BF16)],
        scratch_shapes=[pltpu.VMEM((layers, units, 2, rows, U), BF16), pltpu.SemaphoreType.DMA((2, layers, units))],
        name="prep",
    )(w_gate, w_up, w_down.reshape(layers, units, UB, d))


def layers_kernel(
    x0, dy, wgu_in, wdn_in,
    wgu, wdn, h1, a0T, gate0, up0, fgu, fd,
    squares,
    a1, aT, dyv, acc, hid, dgt, dup, wv, wdv, upt,
    ggu, gd, pgu, pd,
    sa1, ra1, sb1, rb1, sa2, ra2, sb2, rb2, res1, res2,
    sa3, ra3, sb3, rb3, sa4, ra4, sb4, rb4, q1, q2,
    zs1, zs2, zr1, zr2, gz1, gz2, ss, sr,
    wsem, asem, tsem,
    psend, precv, s1s, s1r, s2s, s2r, s3s, s3r, s4s, s4r, zss, zsr, gss, gsr, gls, ys, yr, qss, qsr,
    xas, xar, xbs, xbr, yas, yar, ybs, ybr, dds, ddr,
    *, tile, nz,
):
    tokens, d = dyv.shape
    total_units = wgu.shape[0]
    units = total_units // TWO
    n_tiles = tokens // tile
    ngz = nz - 1
    half = ngz - ngz // TWO

    s, r = lax.axis_index("s"), lax.axis_index("r")
    x, c = lax.div(s, NC), lax.rem(s, NC)
    y, z = lax.div(r, nz), lax.rem(r, nz)
    turn = lambda i, by, n: lax.rem(i + by + n, n)
    x_dev = lambda k: {"s": turn(x, k, NX) * NC + c}
    y_dev = lambda k: {"r": turn(y, k, NY) * nz + z}
    z_dev = lambda k: {"r": y * nz + k}
    partner = {"s": x * NC + 1 - c}
    ways = tuple(enumerate((1, -1)))

    def remote(src, dst, send, recv, dev):
        return Copy(src_ref=src, dst_ref=dst, send_sem=send, recv_sem=recv, device_id=dev, device_id_type=MESH)

    def when(condition, do):
        pl.when(condition)(do)

    barrier = pltpu.get_barrier_semaphore()
    peers = [partner] + [dev(k) for dev in (x_dev, y_dev) for k in range(1, NX)]
    peers += [z_dev(turn(z, k, nz)) for k in range(1, nz)]
    for dev in peers:
        pl.semaphore_signal(barrier, inc=1, device_id=dev, device_id_type=MESH)
    pl.semaphore_wait(barrier, len(peers))

    def cols(k):
        return pl.ds(pl.multiple_of(k * LANES, LANES), LANES)

    def piece(v, k, q):
        return wgu.at[v, :, k, c, :, cols(q)]

    def x_first(v):
        a2 = lax.rem(v, TWO)
        for w, by in ways:
            out = [(piece(v, x, y), 0), (wdn.at[v, x, c], 1)]
            yield by, [remote(ref, ref, xas.at[a2, w, i], xar.at[a2, w, i], x_dev(by)) for ref, i in out]

    def x_second(v):
        a2 = lax.rem(v, TWO)
        for w, by in ways:
            k = turn(x, -by, NX)
            out = [(wgu.at[v, w, k, c, :, cols(y)], 0), (wdn.at[v, k, c, pl.ds(w * (UB // TWO), UB // TWO)], 1)]
            yield by, [remote(ref, ref, xbs.at[a2, w, i], xbr.at[a2, w, i], x_dev(by)) for ref, i in out]

    def y_first(v, which):
        a2 = lax.rem(v, TWO)
        for w, by in ways:
            out = [(piece(v, turn(x, i, NX), y), i) for i in which]
            yield by, [remote(ref, ref, yas.at[a2, w, i], yar.at[a2, w, i], y_dev(by)) for ref, i in out]

    def y_second(v, which):
        a2 = lax.rem(v, TWO)
        for w, by in ways:
            out = [(wgu.at[v, w, turn(x, i, NX), c, :, cols(turn(y, -by, NY))], i) for i in which]
            yield by, [remote(ref, ref, ybs.at[a2, w, i], ybr.at[a2, w, i], y_dev(by)) for ref, i in out]

    def across(v):
        a2 = lax.rem(v, TWO)
        out = [(wgu.at[v, :, :, c], 0), (wdn.at[v, :, c], 1)]
        return [remote(ref, ref, dds.at[a2, i], ddr.at[a2, i], partner) for ref, i in out]

    def every(groups):
        return [copy for _, group in groups for copy in group]

    near, far = (1, NX - 1), (TWO,)

    def g1(v):
        start(every(x_first(v)))

    def g2(v):
        arrived(every(x_first(v)))
        start(every(x_second(v)))
        start(every(y_first(v, near)))

    def g3(v):
        arrived(every(x_second(v)))
        start(every(y_first(v, far)))
        arrived(every(y_first(v, near)))
        start(every(y_second(v, near)))
        sent(every(x_first(v)))

    def g4(v):
        arrived(every(y_first(v, far)))
        start(every(y_second(v, far)))
        arrived(every(y_second(v, near)))
        sent(every(x_second(v)))
        sent(every(y_first(v, near)))

    def g5(v):
        arrived(every(y_second(v, far)))
        start(across(v))
        sent(every(y_first(v, far)))
        sent(every(y_second(v, near)))

    def g6(v):
        arrived(across(v))
        sent(across(v))
        sent(every(y_second(v, far)))
        start(weights(v))

    stages = (g1, g2, g3, g4, g5, g6)

    def gather(t, *numbers):
        for number in numbers:
            v = t - (number - 1)
            when((v >= 0) & (v < total_units), functools.partial(stages[number - 1], v))

    def weights(v, down_only=False):
        slot, unit = lax.rem(v, TWO), lax.rem(v, total_units)
        swap = lax.rem(lax.rem(unit, units), TWO)
        copies = [] if down_only else [pltpu.make_async_copy(wgu.at[unit, h], wv.at[slot, h], wsem.at[slot, h]) for h in BOTH]
        for q in BOTH:
            copies.append(pltpu.make_async_copy(wdn.at[unit, :, q], wdv.at[slot, :, other(q, swap)], wsem.at[slot, TWO + q]))
        return copies

    class Ring:
        def __init__(self, me, dev, get, put, buffers, send, recv):
            self.me, self.get, self.put = me, get, put
            self.sa, self.ra, self.sb, self.rb = buffers
            self.a = [remote(self.sa(w), self.ra(w), send.at[w], recv.at[w], dev(by)) for w, by in ways]
            at = lambda w, h: TWO + TWO * w + h
            self.b = [[remote(self.sb(w, h), self.rb(w, h), send.at[at(w, h)], recv.at[at(w, h)], dev(by)) for h in BOTH] for w, by in ways]

        def start(self):
            for h in BOTH:
                self.sa(h)[...] = self.get(turn(self.me, TWO, FOUR), h).astype(BF16)
                self.a[h].start()
            for w, by in ways:
                self.sb(w, 1 - w)[...] = self.get(turn(self.me, by, FOUR), 1 - w).astype(BF16)
                self.b[w][1 - w].start()

        def middle(self):
            for h, by in ways:
                self.a[h].wait_recv()
                self.sb(h, h)[...] = (self.get(turn(self.me, by, FOUR), h) + self.ra(h)[...].astype(F32)).astype(BF16)
                self.b[h][h].start()
            sent(self.a)

        def end(self):
            for w in BOTH:
                arrived(self.b[w])
            for h in BOTH:
                self.put(h, self.get(self.me, h) + self.rb(0, h)[...].astype(F32) + self.rb(1, h)[...].astype(F32))
            for w in BOTH:
                sent(self.b[w])

    def slots(u):
        return lax.rem(u, TWO), lax.rem(u, THREE), lax.rem(lax.rem(u, units), TWO)

    def ring1(u):
        a2, p, _ = slots(u)

        def get(k, h):
            return ggu[a2, h, k, c].astype(F32) + pgu[p, h, k].astype(F32)

        def put(h, total):
            for k in range(NY):
                res1[k, h] = total[:, k * LANES : (k + 1) * LANES]

        buffers = lambda h: sa1.at[h], lambda h: ra1.at[a2, h], lambda w, h: sb1.at[a2, w, h], lambda w, h: rb1.at[p, w, h]
        return Ring(x, x_dev, get, put, buffers, s1s.at[a2], s1r.at[p])

    def ring2(u):
        a2, p, swap = slots(u)
        pos = other(c, swap)

        def get(k, h):
            return gd[a2, pl.ds(TWO * h, TWO), pos, k].astype(F32) + pd[p, pl.ds(TWO * h, TWO), k].astype(F32)

        def put(h, total):
            res2[pl.ds(TWO * h, TWO)] = total

        buffers = lambda h: sa2.at[h], lambda h: ra2.at[a2, h], lambda w, h: sb2.at[a2, w, h], lambda w, h: rb2.at[p, w, h]
        return Ring(y, y_dev, get, put, buffers, s2s.at[a2], s2r.at[p])

    def ring3(u):
        a2, _, _ = slots(u)

        def get(k, h):
            return res1[k, h]

        def put(h, total):
            rows = total.shape[0] // ngz
            for k in range(ngz):
                q1[k, h] = total[k * rows : (k + 1) * rows]

        buffers = lambda h: sa3.at[h], lambda h: ra3.at[a2, h], lambda w, h: sb3.at[w, h], lambda w, h: rb3.at[a2, w, h]
        return Ring(y, y_dev, get, put, buffers, s3s, s3r.at[a2])

    cut = [pl.ds(0, U), pl.ds(U, d - U)]

    def ring4(u):
        a2, _, _ = slots(u)

        def get(k, h):
            return res2[k, :, cut[h]]

        def put(h, total):
            q2[:, cut[h]] = total

        buffers = lambda h: sa4.at[:, cut[h]], lambda h: ra4.at[a2, :, cut[h]], lambda w, h: sb4.at[w, :, cut[h]], lambda w, h: rb4.at[a2, w, :, cut[h]]
        return Ring(x, x_dev, get, put, buffers, s4s, s4r.at[a2])

    def to_partner(u):
        a2, p, swap = slots(u)
        ends = [(ggu.at[a2, h, :, 1 - c], pgu.at[p, h]) for h in BOTH] + [(gd.at[a2, :, other(1 - c, swap)], pd.at[p])]
        return [remote(src, dst, psend.at[i], precv.at[p, i], partner) for i, (src, dst) in enumerate(ends)]

    def c1(u):
        copies = to_partner(u)
        arrived(copies[:TWO])
        ring1(u).start()
        arrived(copies[TWO:])
        ring2(u).start()
        sent(copies)

    def c2(u):
        ring1(u).middle()
        ring2(u).middle()

    def c3(u):
        ring1(u).end()
        ring3(u).start()
        ring2(u).end()
        ring4(u).start()

    def c4(u):
        ring3(u).middle()
        ring4(u).middle()

    def others(n, do):
        for k in range(n):
            when(k != z, functools.partial(do, k))

    def z_copies(u, k, sender=None):
        a2 = lax.rem(u, TWO)
        sender = z if sender is None else sender
        ends = (zs1.at[k], zr1.at[a2, sender]), (zs2.at[k], zr2.at[a2, sender])
        return [remote(src, dst, zss.at[k, i], zsr.at[a2, sender, i], z_dev(k)) for i, (src, dst) in enumerate(ends)]

    def c5(u):
        ring3(u).end()
        ring4(u).end()
        width = d // ngz
        for k in range(ngz):
            zs1[k] = q1[k].astype(BF16)
            zs2[k] = q2[:, pl.ds(k * width, width)].astype(BF16)
        others(ngz, lambda k: start(z_copies(u, k)))

    def gather_copies(u, k, sender=None):
        a2 = lax.rem(u, TWO)
        sender = z if sender is None else sender
        ends = (gz1, fgu.at[u, y, sender]), (gz2, fd.at[u, y, sender])
        return [remote(src, dst, gss.at[k, i], gsr.at[a2, sender, i], z_dev(k)) for i, (src, dst) in enumerate(ends)]

    def own_copies(u):
        return [pltpu.make_async_copy(gz1, fgu.at[u, y, z], gls.at[0]), pltpu.make_async_copy(gz2, fd.at[u, y, z], gls.at[1])]

    def c6(u):
        a2 = lax.rem(u, TWO)

        def sums():
            others(nz, lambda k: arrived(z_copies(u, 0, k)))
            zone, width = lax.rem(z, ngz), d // ngz
            one, two = q1[zone], q2[:, pl.ds(pl.multiple_of(zone * width, LANES), width)]
            for k in range(nz):
                one += jnp.where(k == z, 0.0, zr1[a2, k].astype(F32))
                two += jnp.where(k == z, 0.0, zr2[a2, k].astype(F32))
            one, two = one.astype(BF16), two.astype(BF16)
            gz1[...], gz2[...] = one, two
            one, two = one.astype(F32), two.astype(F32)
            ss[...] += jnp.full(ss.shape, jnp.sum(one * one) + jnp.sum(two * two))
            start(own_copies(u))
            others(nz, lambda k: start(gather_copies(u, k)))

        when(z < ngz, sums)
        others(ngz, lambda k: sent(z_copies(u, k)))

    def y_copies(u, by, second, sender_y=None):
        a2 = lax.rem(u, TWO)
        w = 0 if by > 0 else 1
        if not second:
            ends = fgu.at[u, y], fd.at[u, y]
        else:
            k = turn(y, -by, NY)
            ends = fgu.at[u, k, :, w], fd.at[u, k, (pl.ds(0, half), pl.ds(half, ngz - half))[w]]
        return [remote(ref, ref, ys.at[w, second, i], yr.at[a2, w, second, i], y_dev(by)) for i, ref in enumerate(ends)]

    def c7(u):
        others(ngz, lambda k: arrived(gather_copies(u, 0, k)))

        def mine():
            done(own_copies(u))
            others(nz, lambda k: sent(gather_copies(u, k)))

        when(z < ngz, mine)
        for _, by in ways:
            start(y_copies(u, by, 0))

    def c8(u):
        for _, by in ways:
            arrived(y_copies(u, by, 0))
            start(y_copies(u, by, 1))

    def c9(u):
        for _, by in ways:
            arrived(y_copies(u, by, 1))
            sent(y_copies(u, by, 0))
            sent(y_copies(u, by, 1))

    plan = {0: ((c5, THREE), (c7, FOUR)), 1: ((c1, 1),), 2: ((c3, TWO), (c8, FOUR)), 3: ((c6, THREE), (c4, TWO)), 4: ((c2, 1), (c9, FOUR))}

    def steps(t, place):
        for step, behind in plan[place]:
            u = t - behind
            when((u >= 0) & (u < total_units), functools.partial(step, u))

    def rows_of(i):
        return pl.ds(pl.multiple_of(i * tile, tile), tile)

    def weight_gradients(t):
        a2 = lax.rem(t, TWO)
        copies = to_partner(t)
        for h, by in enumerate((dgt, dup)):
            ggu[a2, h] = nn(aT[...], by[...]).astype(BF16).reshape(ggu.shape[TWO:])
            copies[h].start()
            steps(t, THREE + h)
        gd[a2] = tn(hid[...], dyv[...]).astype(BF16).reshape(gd.shape[1:])
        copies[TWO].start()

    load = pltpu.make_async_copy(x0, dyv, asem.at[0])
    load.start()
    gather(0, 1)
    ss[...] = jnp.zeros(ss.shape, F32)
    load.wait()
    keep = pltpu.make_async_copy(aT, a0T, asem.at[1])

    def norm(i, _):
        rows = rows_of(i)
        wide = dyv[rows].astype(F32)
        wide = wide * scale_of(wide)
        a1[rows] = wide.astype(BF16)
        aT[:, rows] = wide.T.astype(BF16)
        acc[0, rows] = jnp.zeros((tile, d), F32)
        return 0

    lax.fori_loop(0, n_tiles, norm, 0)
    keep.start()

    def fill(t, _):
        gather(t, 6, 5, 4, 3, 2, 1)
        return 0

    lax.fori_loop(1, SIX, fill, 0)

    def out_tile(j, i):
        slot = i % TWO
        at = pl.ds(slot * tile, tile)
        return [pltpu.make_async_copy(acc.at[1, at, pl.ds(0, U)], gate0.at[j, pl.ds(i * tile, tile)], tsem.at[slot, 0]),
                pltpu.make_async_copy(upt.at[at], up0.at[j, pl.ds(i * tile, tile)], tsem.at[slot, 1])]

    def forward(j, _):
        t = j + SIX
        slot = lax.rem(j, TWO)
        gather(t, 6)
        done(weights(j))
        w_g, w_u, w_d = wv[slot, 0].reshape(d, U), wv[slot, 1].reshape(d, U), wdv[slot].reshape(U, d)
        for i in range(n_tiles):
            rows = pl.ds(i * tile, tile)
            at = pl.ds(i % TWO * tile, tile)
            if i < TWO:
                when(j > 0, lambda: done(out_tile(j, i)))
            else:
                done(out_tile(j, i))
            g, u = nn(a1[rows], w_g), nn(a1[rows], w_u)
            acc[1, at, pl.ds(0, U)], upt[at] = g, u
            start(out_tile(j, i))
            acc[0, rows] += nn((g * jax.nn.sigmoid(g) * u).astype(BF16), w_d)
            gather(t, *((5,), (4, 3), (2, 1), ())[i])
        return 0

    lax.fori_loop(0, units, forward, 0)
    for i in range(min(TWO, n_tiles)):
        done(out_tile(0, i))
    keep.wait()

    def between(i, _):
        rows = rows_of(i)
        h = dyv[rows] + acc[0, rows].astype(BF16)
        hid[rows], dgt[rows, cut_low] = h[:, :U], h[:, U:]
        pltpu.make_async_copy(dy.at[rows], dyv.at[rows], asem.at[0]).start()
        wide = h.astype(F32)
        wide = wide * scale_of(wide)
        a1[rows] = wide.astype(BF16)
        aT[:, rows] = wide.T.astype(BF16)
        for h in BOTH:
            acc[h, rows] = jnp.zeros((tile, d), F32)
        return 0

    cut_low = pl.ds(0, d - U)
    lax.fori_loop(0, n_tiles, between, 0)
    keep = [pltpu.make_async_copy(hid, h1.at[:, cut[0]], asem.at[1]), pltpu.make_async_copy(dgt.at[:, cut_low], h1.at[:, cut[1]], asem.at[TWO])]
    start(keep)
    pltpu.make_async_copy(dy, dyv, asem.at[0]).wait()
    done(keep)

    def both_passes(t, _):
        v = t + units
        slot = lax.rem(v, TWO)
        steps(t, 0)
        gather(v + SIX, 6, 5, 4)
        when(t == units - 1, lambda: start(weights(total_units, True)))
        done(weights(v))
        w_g, w_u, w_d = wv[slot, 0].reshape(d, U), wv[slot, 1].reshape(d, U), wdv[slot].reshape(U, d)
        for i in range(n_tiles):
            rows = pl.ds(i * tile, tile)
            g, u = nn(a1[rows], w_g), nn(a1[rows], w_u)
            dh = nt(dyv[rows], w_d).astype(BF16).astype(F32)
            hid[rows], by_gate, by_up = glu_backward(g, u, dh)
            dgt[rows], dup[rows] = by_gate, by_up
            acc[0, rows] += nt(by_up, w_u)
            acc[1, rows] += nt(by_gate, w_g)
            if i == min(1, n_tiles - 1):
                steps(t, 1)
                gather(v + SIX, 3, 2, 1)
        steps(t, TWO)
        weight_gradients(t)
        return 0

    lax.fori_loop(0, units, both_passes, 0)

    loads = [pltpu.make_async_copy(h1, a1, asem.at[0]), pltpu.make_async_copy(a0T, aT, asem.at[1])]
    start(loads)
    loads[0].wait()

    def cotangent(i, _):
        rows = rows_of(i)
        wide = a1[rows].astype(F32)
        scale = scale_of(wide)
        by_a = (acc[0, rows].astype(BF16).astype(F32) + acc[1, rows].astype(BF16).astype(F32)).astype(BF16).astype(F32)
        inner = jnp.sum(wide * by_a, -1, keepdims=True)
        by_h = by_a * scale - wide * (inner * (scale * scale * scale) * (1.0 / d))
        dyv[rows] = (dyv[rows].astype(F32) + by_h.astype(BF16).astype(F32)).astype(BF16)
        return 0

    lax.fori_loop(0, n_tiles, cotangent, 0)
    loads[1].wait()

    def in_tile(j, i):
        rows = pl.ds(i * tile, tile)
        ends = (gate0, 0), (up0, 1)
        return [pltpu.make_async_copy(src.at[j, rows], acc.at[h, rows, pl.ds(0, U)], tsem.at[TWO + i, h]) for src, h in ends]

    for i in range(n_tiles):
        start(in_tile(0, i))

    def backward_only(t, _):
        j = t - units
        v = t + units
        slot = lax.rem(v, TWO)
        steps(t, 0)
        when(j < units - 1, lambda: start(weights(v + 1, True)))
        done(weights(v, True))
        w_d = wdv[slot].reshape(U, d)
        for i in range(n_tiles):
            rows = pl.ds(i * tile, tile)
            done(in_tile(j, i))
            dh = nt(dyv[rows], w_d).astype(BF16).astype(F32)
            hid[rows], dgt[rows], dup[rows] = glu_backward(acc[0, rows, pl.ds(0, U)], acc[1, rows, pl.ds(0, U)], dh)
            if i == min(1, n_tiles - 1):
                steps(t, 1)
        steps(t, TWO)

        def ahead():
            for i in range(n_tiles):
                start(in_tile(j + 1, i))

        when(j < units - 1, ahead)
        weight_gradients(t)
        return 0

    lax.fori_loop(units, total_units, backward_only, 0)

    for t in range(THREE):
        for place in plan:
            steps(total_units + t, place)

    def exchange(number, devs):
        copies = [remote(ss, sr.at[number, i], qss.at[number, i], qsr.at[number, i], dev) for i, dev in enumerate(devs)]
        start(copies)

        def finish():
            arrived(copies)
            sent(copies)
            total = ss[...]
            for i in range(len(devs)):
                total += sr[number, i]
            ss[...] = total

        return finish

    last = total_units - 1
    finish = exchange(0, [z_dev(turn(z, k, nz)) for k in range(1, nz)])
    finish()
    finish = exchange(1, [y_dev(k) for k in range(1, NY)])
    c7(last)
    finish()
    finish = exchange(TWO, [x_dev(k) for k in range(1, NX)])
    c8(last)
    finish()
    finish = exchange(THREE, [partner])
    c9(last)
    finish()
    squares[...] = ss[...]


def layers(x, dy, wgu, wdn, nz):
    tokens, d = x.shape
    units = wgu.shape[0] // TWO
    tile = TILE
    n_tiles = tokens // tile
    rg, ngz = d // S, nz - 1
    rz, cz, rd = rg // ngz, d // ngz, UB // NY
    vmem = lambda *shape, dtype=BF16: pltpu.VMEM(shape, dtype)
    slots = lambda *shape: [vmem(*lead, *shape) for lead in ((TWO,), (TWO, TWO), (TWO, TWO, TWO), (THREE, TWO, TWO))]
    small = lambda *shape: [vmem(*lead, *shape) for lead in ((TWO,), (TWO, TWO), (TWO, TWO), (TWO, TWO, TWO))]
    narrow = lambda *shape: [vmem(*lead, *shape) for lead in ((), (TWO,), (TWO,), (TWO, TWO))]
    dma = lambda *shape: pltpu.SemaphoreType.DMA(shape)
    scratch = [
        vmem(tokens, d), vmem(d, tokens), vmem(tokens, d), vmem(TWO, tokens, d, dtype=F32),
        vmem(tokens, U), vmem(tokens, U), vmem(tokens, U),
        vmem(TWO, TWO, NX, NC, rg, U), vmem(TWO, NX, NC, UB, d), vmem(min(TWO, n_tiles) * tile, U, dtype=F32),
        vmem(TWO, TWO, NX, NC, rg, U), vmem(TWO, NX, NC, NY, rd, d), vmem(THREE, TWO, NX, rg, U), vmem(THREE, NX, NY, rd, d),
        *slots(rg, U), *slots(TWO, rd, d),
        vmem(NY, TWO, rg, LANES, dtype=F32), vmem(NX, rd, d, dtype=F32),
        *small(rg, LANES), *narrow(rd, d),
        vmem(ngz, TWO, rz, LANES, dtype=F32), vmem(rd, d, dtype=F32),
        vmem(ngz, TWO, rz, LANES), vmem(ngz, rd, cz), vmem(TWO, nz, TWO, rz, LANES), vmem(TWO, nz, rd, cz),
        vmem(TWO, rz, LANES), vmem(rd, cz), vmem(S, LANES, dtype=F32), vmem(FOUR, max(nz, NX), S, LANES, dtype=F32),
        dma(TWO, FOUR), dma(THREE), dma(TWO + n_tiles, TWO),
        dma(THREE), dma(THREE, THREE), dma(TWO, SIX), dma(THREE, SIX), dma(TWO, SIX), dma(THREE, SIX), dma(SIX), dma(TWO, SIX), dma(SIX), dma(TWO, SIX),
        dma(ngz, TWO), dma(TWO, nz, TWO), dma(nz, TWO), dma(TWO, nz, TWO), dma(TWO), dma(TWO, TWO, TWO), dma(TWO, TWO, TWO, TWO), dma(FOUR, nz), dma(FOUR, nz),
        dma(TWO, TWO, TWO), dma(TWO, TWO, TWO), dma(TWO, TWO, TWO), dma(TWO, TWO, TWO), dma(TWO, TWO, NX), dma(TWO, TWO, NX), dma(TWO, TWO, NX), dma(TWO, TWO, NX), dma(TWO, TWO), dma(TWO, TWO),
    ]
    anywhere = pl.BlockSpec(memory_space=pl.ANY)
    array = jax.ShapeDtypeStruct
    return pl.pallas_call(
        functools.partial(layers_kernel, tile=tile, nz=nz),
        in_specs=[anywhere] * FOUR,
        out_specs=[anywhere] * S + [pl.BlockSpec(memory_space=pltpu.VMEM)],
        out_shape=[
            array(wgu.shape, BF16),
            array(wdn.shape, BF16),
            array((tokens, d), BF16),
            array((d, tokens), BF16),
            array((units, tokens, U), F32),
            array((units, tokens, U), F32),
            array((TWO * units, NY, ngz, TWO, rz, LANES), BF16),
            array((TWO * units, NY, ngz, rd, cz), BF16),
            array((S, LANES), F32),
        ],
        scratch_shapes=scratch,
        input_output_aliases={TWO: 0, THREE: 1},
        compiler_params=pltpu.CompilerParams(collective_id=1, has_side_effects=True, vmem_limit_bytes=67043328),
        cost_estimate=pl.CostEstimate(flops=15 * TWO * tokens * d * U * units, bytes_accessed=2**28, transcendentals=0),
        name="layers",
    )(x, dy, wgu, wdn)[SIX:]


def step_kernel(squares, fgu, fd, wg, mg, vg, wu, mu, vu, wd, md, vd, *out, n_units, count):
    ngz, rd, cz = fd.shape[2:]
    fac = jnp.minimum(1.0, 0.5 * lax.rsqrt(squares[0:1] / count + 1e-30))[:, 0:1]

    def adamw(g, w, m, v):
        g = g.astype(F32) * fac
        m = 0.9 * m + 0.1 * g
        v = 0.95 * v + 0.05 * g * g
        step = m * lax.rsqrt(v + 1e-8) + 0.1 * w.astype(F32)
        return (w.astype(F32) - 0.02 * step).astype(BF16), m, v

    rows = wg.shape[1]
    low = lax.broadcasted_iota(jnp.int32, (rows, LANES), 1) < UB
    for h, (w, m, v, outs) in enumerate(((wg, mg, vg, out[0::THREE]), (wu, mu, vu, out[1::THREE]))):
        by_unit = [jnp.concatenate([fgu[j, 0, k, h] for k in range(ngz)], axis=0).astype(F32) for j in range(n_units)]
        for i in range(n_units):
            at = pl.ds(i * LANES, LANES)
            g = jnp.where(low, by_unit[TWO * i % n_units], by_unit[(TWO * i + 1) % n_units])
            outs[0][0, :, at], outs[1][0, :, at], outs[2][0, :, at] = adamw(g, w[0, :, at], m[0, :, at], v[0, :, at])
    outs = out[TWO::THREE]
    for j in range(n_units):
        g = jnp.concatenate([fd[j, 0, k] for k in range(ngz)], axis=1)
        outs[0][0, j, 0], outs[1][0, j, 0], outs[2][0, j, 0] = adamw(g, wd[0, j, 0], md[0, j, 0], vd[0, j, 0])


def optimizer(squares, fgu, fd, weights, m, v):
    layers, rg, ff = weights[0].shape
    n_units = ff // U
    d = weights[2].shape[2]
    _, _, ngz, rd, cz = fd.shape
    rz = rg // ngz
    wide = ff // NY
    down = lambda a: a.reshape(layers, n_units, NY, rd, d)
    col = pl.BlockSpec((1, rg, wide), lambda l, a: (l, 0, a))
    row = pl.BlockSpec((1, n_units, 1, rd, d), lambda l, a: (l, 0, a, 0, 0))
    args = []
    for i in range(3):
        args += [w if i < 2 else down(w) for w in (weights[i], m[i], v[i])]
    shapes = lambda dtype: [jax.ShapeDtypeStruct((layers, rg, ff), dtype)] * 2 + [jax.ShapeDtypeStruct((layers, n_units, NY, rd, d), dtype)]
    out = pl.pallas_call(
        functools.partial(step_kernel, n_units=n_units, count=S * sum(w.size for w in weights)),
        grid=(layers, NY),
        in_specs=[
            pl.BlockSpec((S, LANES), lambda l, a: (0, 0)),
            pl.BlockSpec((n_units, 1, ngz, 2, rz, LANES), lambda l, a: (1 - l, a, 0, 0, 0, 0)),
            pl.BlockSpec((n_units, 1, ngz, rd, cz), lambda l, a: (1 - l, a, 0, 0, 0)),
        ]
        + [col] * 6
        + [row] * 3,
        out_specs=[col, col, row] * 3,
        out_shape=shapes(BF16) + shapes(F32) + shapes(F32),
        name="adamw",
    )(squares, fgu, fd, *args)
    return tuple(o.reshape(layers, -1, d) if i % 3 == 2 else o for i, o in enumerate(out))


def solution(mesh):
    nz = mesh.shape["r"] // NY

    def step(x, dy, *arrays):
        weights, m, v = (arrays[i : i + THREE] for i in (0, THREE, SIX))
        fgu, fd, squares = layers(x[0], dy[0], *prep(*weights), nz)
        return optimizer(squares, fgu, fd, weights, m, v)

    states, cut = P(("rep", "r", "s"), None, None), P(None, "s", None)
    return jax.shard_map(
        step,
        mesh=mesh,
        in_specs=(states, states) + (cut,) * 9,
        out_specs=(P("rep", "s", None),) * 9,
        check_vma=False,
    )
```

time: 916 us -> 441 us (0.48)
  waiting for transfers between devices: 441 us -> 0 us
  Pallas kernels: 0 us -> 432 us
  matrix products: 380 us -> 0 us
  other arithmetic: 30 us -> 0 us
  local copies, waits for them, and re-layouts: 25.4 us -> 0 us
  between operations: 17 us -> 0.86 us
  blocking collectives: 14.6 us -> 0 us
    pallas_call x0 -> x3, Pallas kernels: none -> 432 us  [the longest x1 407 us: layers(): pl.pallas_call(functools.partial(layers_kernel, tile=tile, nz=nz), in_spe...]
    dot_general x15 -> x0, matrix products: 380 us -> none  [the longest x5 140 us: layer(): gate = jnp.dot(a, w['w_gate'], preferred_element_type=jnp.float32)]
    psum x1 -> x0, waiting for transfers between devices: 172 us -> none  [summed(): lax.psum(lax.psum_scatter(term, 's', scatter_dimension=0, tiled=True), 'r')]
    reduce_scatter x6 -> x0, waiting for transfers between devices: 134 us -> none  [summed(): lax.psum_scatter(term, 's', scatter_dimension=0, tiled=True)]
    all_gather x6 -> x0, waiting for transfers between devices: 133 us -> none  [fetched(): lax.all_gather(w[number], 's', axis=0, tiled=True)]
    unnamed x42 -> x0, local copies, waits for them, and re-layouts: 18.7 us -> none
    convert_element_type x2 -> x0, other arithmetic: 15.7 us -> none  [adamw(): return ((w - 0.02 * step).astype(jnp.bfloat16), m, v)]
    psum x1 -> x0, blocking collectives: 14.6 us -> none  [step(): squares = lax.psum(sum((jnp.sum(g * g) for g in gradients)), 's')]
  transfers between devices with their start and end apart: 13 -> 0, of which waited for: 10 -> 0; matrix products, arithmetic and copies ran while one was open for 32% -> 0% of each run, Pallas kernels for 0% -> 0%
where the time goes in v2:
time: 441 us; the launch traced here: 433 us
  Pallas kernels  432 us (98%)
    pallas_call x1, Pallas kernels, layers(): pl.pallas_call(functools.partial(layers_kernel, tile=tile, nz=nz), in_spe...  407 us
    pallas_call x1, Pallas kernels, optimizer(): pl.pallas_call(functools.partial(step_kernel, n_units=n_units, count=S *...  20.1 us

profile of v2, /device:TPU:1, one launch (start us, length us, event | category | flops | bytes accessed | tf_op | source)
XLA Modules:
  0.0 433.3 jit_solution(15011713409641146796)
XLA Ops:
  0.6 4.9 %prep.1 = (bf16[14,2,4,2,112,512]{5,4,3,2,1,0:T(8,128)(2,1)}, bf16[14,4,2,64,896]{4,3,2,1,0:T(8,128)(2,1)}) custom-call(bf16[2,112,3584]{2,1,0:T(8,128)(2,1)} %wg.3, bf16[2,112,3584]{2,1,0:T(8,128)(2,1)} %wu.3, bf16[2,7,64,896]{3,2,1,0:T(8,128)(2,1)} %bitcast.9), custom_call_target="tpu_custom_call" | custom-call | tf_op jit(solution)/shard_map/prep/pallas_call | solution.py:108
  5.5 407.4 %layers.1 = (bf16[14,2,4,2,112,512]{5,4,3,2,1,0:T(8,128)(2,1)}, bf16[14,4,2,64,896]{4,3,2,1,0:T(8,128)(2,1)}, bf16[2048,896]{1,0:T(8,128)(2,1)}, bf16[896,2048]{...) custom-call(bf16[2048,896]{1,0:T(8,128)(2,1)} %bitcast.13, ...), custom_call_target="tpu_custom_call", output_to_operand_aliasing={{0}: (2, {}), {1}: (3, {})} | custom-call | flops 197300060160 | bytes 268435456 | tf_op jit(solution)/shard_map/layers/pallas_call | solution.py:683
  413.0 20.1 %adamw.1 = (bf16[2,112,3584]{2,1,0:T(8,128)(2,1)}, bf16[2,112,3584]{2,1,0:T(8,128)(2,1)}, bf16[2,7,4,16,896]{4,3,2,1,0:T(8,128)(2,1)}, f32[2,112,3584]{2,1,0:T(8...) custom-call(f32[8,128]{1,0:T(8,128)} %get-tuple-element.25.squares, ...), custom_call_target="tpu_custom_call" | custom-call | tf_op jit(solution)/shard_map/adamw/pallas_call | solution.py:745
